TPU v7x, 256 devices: a whole 4x4x8 slice. The times are simulated.
256 devices in a mesh: expert: 8 (over x, core), ffn: 32 (over z, y).
Axes of the slice: x: 4, y: 4, z: 8, core: 2. Of those that a mesh axis runs over, the one named last changes fastest.
Arguments:
- tokens: bfloat16 [8, 128, 4096], P('expert', 'ffn'), may hold values from -6 to 6
- routes: int32 [8, 128, 2], P('expert'), may hold values from 0 to 7, all different within a row; in each aligned block of 128 rows (0 to 127, 128 to 255, ..., all dimensions but the last counted through in order) at most 48 rows name the same one
- router: bfloat16 [4096, 8], replicated, may hold values from -0.09375 to 0.09375
- w_gate: bfloat16 [8, 4096, 12288], P('expert', None, 'ffn'), may hold values from -0.09375 to 0.09375
- w_up: bfloat16 [8, 4096, 12288], P('expert', None, 'ffn'), may hold values from -0.09375 to 0.09375
- w_down: bfloat16 [8, 12288, 4096], P('expert', 'ffn'), may hold values from -0.109375 to 0.109375
- adapter: bfloat16 [8, 4096, 4096], P('expert', None, 'ffn'), may hold values from -0.09375 to 0.09375
- upstream: bfloat16 [8, 128, 4096], P('expert', None, 'ffn'), may hold values from -24 to 24
- bound: float32 [8], P('expert'), may hold values from 2048 to 16384
Outputs:
- adapted: bfloat16 [8, 128, 4096], P('expert', None, 'ffn')
- clipped: bfloat16 [8, 4096, 4096], P('expert', None, 'ffn')
Inputs may be any that keep to these rules, and one draw needn't show every extreme that they name: `routes`: each token names two different experts; for each client at most 48 of its tokens name any one expert, and in some clients some expert is named by exactly 48 tokens.
All inputs are finite; a program needn't handle non-finite values.
Results may differ from a plain program's by a relative error of at most 0.015.
Values may be sent and summed in bfloat16 or wider, within the bound.
A program may use at most 64 MiB of HBM per device.

v0:
```python
import functools

import jax
import jax.numpy as jnp
from jax import lax
from jax.experimental import pallas as pl
from jax.experimental.pallas import tpu as pltpu
from jax.sharding import PartitionSpec as P

MESH = pl.DeviceIdType.MESH
CORES = 2


def tile_of(size, choices=(512, 384, 256, 128)):
    for width in choices:
        if size % width == 0:
            return width
    return size


def layer_kernel(
    dims,
    tok_ref, routes_ref, router_ref, wg_hbm, wu_hbm, wd_hbm, ad_hbm, up_ref, bound_ref,
    layer_ref, adapted_ref, factor_ref,
    wg, wu, wd, ad, tokbuf, tokc, gate_acc, up_acc, hid, logit_acc, routes_buf, gram_buf,
    sbuf, r1, s2, r2, s3, r3, lbuf,
    w_sem, own_sem, rt_send, rt_recv, gr_send, gr_recv, tf_send, tf_recv, tx_send, tx_recv,
    tc_send, tc_recv, a_send, a_recv, b_send, b_recv, c_send, c_recv, d_send, d_recv,
):
    E, F, KC, NC, D, FFD, t, tl, cd = dims
    X = E // CORES
    T = E * t
    KW = D // KC
    NW = D // NC
    CW = NW // F
    e = lax.axis_index("expert")
    f = lax.axis_index("ffn")
    x, core = e // CORES, lax.rem(e, CORES)
    mate = x * CORES + (CORES - 1 - core)

    loads = {}
    for k in range(KC):
        loads["g", k] = pltpu.make_async_copy(
            wg_hbm.at[pl.ds(k * KW, KW), :], wg.at[k], w_sem.at[0, k]
        )
        loads["u", k] = pltpu.make_async_copy(
            wu_hbm.at[pl.ds(k * KW, KW), :], wu.at[k], w_sem.at[1, k]
        )
    for j in range(NC):
        loads["d", j] = pltpu.make_async_copy(
            wd_hbm.at[:, pl.ds(j * NW, NW)], wd.at[j], w_sem.at[2, j]
        )
    loads["a", 0] = pltpu.make_async_copy(ad_hbm, ad, w_sem.at[3, 0])
    for load in loads.values():
        load.start()
    own = []
    for k in range(KC):
        copy = pltpu.make_async_copy(
            tok_ref.at[:, pl.ds(k * KW, KW)], tokbuf.at[k, e, f], own_sem.at[k]
        )
        copy.start()
        own.append(copy)
    own_routes = pltpu.make_async_copy(routes_ref, routes_buf.at[e], own_sem.at[KC])
    own_routes.start()
    gram_buf[f] = lax.dot_general(
        up_ref[...], up_ref[...], (((1,), (1,)), ((), ())), preferred_element_type=jnp.float32
    )

    barrier = pltpu.get_barrier_semaphore()
    for d in range(1, F):
        pl.semaphore_signal(
            barrier, inc=1, device_id={"ffn": lax.rem(f + d, F)}, device_id_type=MESH
        )
    for d in range(1, E):
        pl.semaphore_signal(
            barrier, inc=1, device_id={"expert": lax.rem(e + d, E)}, device_id_type=MESH
        )
    pl.semaphore_wait(barrier, F + E - 2)

    sent = []

    def send(src, dst, send_sem, recv_sem, device):
        copy = pltpu.make_async_remote_copy(
            src_ref=src, dst_ref=dst, send_sem=send_sem, recv_sem=recv_sem,
            device_id=device, device_id_type=MESH,
        )
        copy.start()
        sent.append(copy)

    def receive(dst, send_sem, recv_sem, device):
        pltpu.make_async_remote_copy(
            src_ref=dst, dst_ref=dst, send_sem=send_sem, recv_sem=recv_sem,
            device_id=device, device_id_type=MESH,
        ).wait_recv()

    def ffn_to(d):
        return {"ffn": lax.rem(f + d, F)}

    def ffn_from(d):
        return lax.rem(f + F - d, F)

    def x_to(d):
        return lax.rem(x + d, X)

    def x_from(d):
        return lax.rem(x + X - d, X)

    for k in range(KC):
        for d in range(1, F):
            send(
                tok_ref.at[:, pl.ds(k * KW, KW)], tokbuf.at[k, e, f],
                tf_send.at[k, d], tf_recv.at[k, d], ffn_to(d),
            )
    for d in range(1, E):
        send(
            routes_ref, routes_buf.at[e], rt_send.at[d], rt_recv.at[d],
            {"expert": lax.rem(e + d, E)},
        )
    for d in range(1, F):
        send(gram_buf.at[f], gram_buf.at[f], gr_send.at[d], gr_recv.at[d], ffn_to(d))

    def forward_client(k):
        own[k].wait()
        for d in range(1, F):
            receive(
                tokbuf.at[k, e, ffn_from(d)], tf_send.at[k, d], tf_recv.at[k, d], ffn_to(d)
            )
        for d in range(1, X):
            send(
                tokbuf.at[k, e], tokbuf.at[k, e], tx_send.at[k, d], tx_recv.at[k, d],
                {"expert": x_to(d) * CORES + core},
            )
        send(
            tokbuf.at[k, e], tokbuf.at[k, e], tc_send.at[k, 0], tc_recv.at[k, 0],
            {"expert": mate},
        )

    def forward_x(k):
        for d in range(1, X):
            block = x_from(d) * CORES + core
            receive(
                tokbuf.at[k, block], tx_send.at[k, d], tx_recv.at[k, d], {"expert": block}
            )
            send(
                tokbuf.at[k, block], tokbuf.at[k, block], tc_send.at[k, d], tc_recv.at[k, d],
                {"expert": mate},
            )

    FT = tile_of(FFD)

    def expand(k):
        for d in range(X):
            block = x_from(d) * CORES + (CORES - 1 - core)
            receive(
                tokbuf.at[k, block], tc_send.at[k, d], tc_recv.at[k, d], {"expert": mate}
            )

        def compact(c, carry):
            rows = jnp.concatenate(
                [tokbuf[k, c, i].astype(jnp.float32) for i in range(F)], axis=0
            ).astype(jnp.bfloat16)
            tokc[k, pl.ds(pl.multiple_of(c * t, t), t), :] = rows
            return carry

        lax.fori_loop(0, E, compact, 0)
        loads["g", k].wait()
        loads["u", k].wait()

        def hidden_tile(i, carry):
            cols = pl.ds(pl.multiple_of(i * FT, FT), FT)
            g = jnp.dot(tokc[k], wg[k, :, cols], preferred_element_type=jnp.float32)
            u = jnp.dot(tokc[k], wu[k, :, cols], preferred_element_type=jnp.float32)
            if k > 0:
                g = gate_acc[:, cols] + g
                u = up_acc[:, cols] + u
            if k < KC - 1:
                gate_acc[:, cols] = g
                up_acc[:, cols] = u
            else:
                hid[:, cols] = (g / (1.0 + jnp.exp(-g)) * u).astype(jnp.bfloat16)
            return carry

        lax.fori_loop(0, FFD // FT, hidden_tile, 0)
        part = lax.dot_general(
            tokc[k], router_ref[:, pl.ds(k * KW, KW)], (((1,), (1,)), ((), ())),
            preferred_element_type=jnp.float32,
        )
        logit_acc[...] = part if k == 0 else logit_acc[...] + part

    for step in range(KC + 2):
        if step < KC:
            forward_client(step)
        if 0 <= step - 1 < KC:
            forward_x(step - 1)
        if 0 <= step - 2:
            expand(step - 2)

    own_routes.wait()
    for d in range(1, E):
        receive(
            routes_buf.at[lax.rem(e + E - d, E)], rt_send.at[d], rt_recv.at[d],
            {"expert": lax.rem(e + d, E)},
        )
    diagonal = lax.broadcasted_iota(jnp.int32, (t, t), 0) == lax.broadcasted_iota(
        jnp.int32, (t, t), 1
    )

    def choice(k):
        named = [routes_buf[c][k:k + 1, :].astype(jnp.float32) for c in range(E)]
        return jnp.concatenate(
            [jnp.sum(jnp.where(diagonal, row, 0.0), axis=1, keepdims=True) for row in named],
            axis=0,
        ).astype(jnp.int32)

    first, second = choice(0), choice(1)
    logits = logit_acc[...]
    expert_ids = lax.broadcasted_iota(jnp.int32, (T, E), 1)
    picked_first = jnp.sum(jnp.where(expert_ids == first, logits, 0.0), axis=1, keepdims=True)
    picked_second = jnp.sum(jnp.where(expert_ids == second, logits, 0.0), axis=1, keepdims=True)
    weight_first = 1.0 / (1.0 + jnp.exp(picked_second - picked_first))
    share = jnp.where(first == e, weight_first, 0.0) + jnp.where(
        second == e, 1.0 - weight_first, 0.0
    )

    NT = tile_of(NW, (256, 128))

    def down(j):
        loads["d", j].wait()
        for n in range(NW // NT):
            value = jnp.dot(
                hid[...], wd[j, :, n * NT:(n + 1) * NT], preferred_element_type=jnp.float32
            )
            value = (value * share).astype(jnp.bfloat16)
            for c in range(E):
                for q in range(NT // CW):
                    sbuf[j, c % CORES, c // CORES, n * (NT // CW) + q] = value[
                        c * t:(c + 1) * t, q * CW:(q + 1) * CW
                    ]
        send(
            sbuf.at[j, CORES - 1 - core], r1.at[j], a_send.at[j], a_recv.at[j],
            {"expert": mate},
        )

    def add_mate(j):
        receive(r1.at[j], a_send.at[j], a_recv.at[j], {"expert": mate})
        for d in range(1, X + 1):
            to = x_to(d)
            s2[j, to] = (
                sbuf[j, core, to].astype(jnp.float32) + r1[j, to].astype(jnp.float32)
            ).astype(jnp.bfloat16)
            if d < X:
                send(
                    s2.at[j, to], r2.at[j, d], b_send.at[j, d], b_recv.at[j, d],
                    {"expert": to * CORES + core},
                )

    def add_x(j):
        total = s2[j, x].astype(jnp.float32)
        for d in range(1, X):
            receive(
                r2.at[j, d], b_send.at[j, d], b_recv.at[j, d],
                {"expert": x_from(d) * CORES + core},
            )
            total = total + r2[j, d].astype(jnp.float32)
        s3[j] = total.astype(jnp.bfloat16)
        for d in range(1, F):
            send(
                s3.at[j, lax.rem(f + d, F)], r3.at[j, d], c_send.at[j, d], c_recv.at[j, d],
                ffn_to(d),
            )

    def add_ffn(j):
        total = s3[j, f].astype(jnp.float32)
        for d in range(1, F):
            receive(r3.at[j, d], c_send.at[j, d], c_recv.at[j, d], ffn_to(d))
            total = total + r3[j, d].astype(jnp.float32)
        start = j * NW
        column = pl.multiple_of(lax.rem(start, KW) + f * CW, CW)
        rows = pl.ds(pl.multiple_of(e * t, t), t)
        if NW <= KW:
            mine = tokc[start // KW, rows, pl.ds(column, CW)]
        else:
            place = start + f * CW
            mine = tokc[place // KW, rows, pl.ds(pl.multiple_of(lax.rem(place, KW), CW), CW)]
        lbuf[j, f] = (mine.astype(jnp.float32) + total).astype(jnp.bfloat16)
        for d in range(1, F):
            send(lbuf.at[j, f], lbuf.at[j, f], d_send.at[j, d], d_recv.at[j, d], ffn_to(d))

    for step in range(NC + 5):
        if step < NC:
            down(step)
        if 0 <= step - 1 < NC:
            add_mate(step - 1)
        if 0 <= step - 3 < NC:
            add_x(step - 3)
        if 0 <= step - 5 < NC:
            add_ffn(step - 5)

    for d in range(1, F):
        receive(gram_buf.at[ffn_from(d)], gr_send.at[d], gr_recv.at[d], ffn_to(d))
    whole_gram = jnp.sum(gram_buf[...], axis=0)
    loads["a", 0].wait()
    layer_gram = jnp.zeros((t, t), jnp.float32)
    adapted = jnp.zeros((t, cd), jnp.float32)
    for j in range(NC):
        for d in range(1, F):
            receive(lbuf.at[j, ffn_from(d)], d_send.at[j, d], d_recv.at[j, d], ffn_to(d))
        block = jnp.concatenate([lbuf[j, i] for i in range(F)], axis=1)
        layer_ref[:, j * NW:(j + 1) * NW] = block
        layer_gram = layer_gram + lax.dot_general(
            block, block, (((1,), (1,)), ((), ())), preferred_element_type=jnp.float32
        )
        adapted = adapted + jnp.dot(
            block, ad[j * NW:(j + 1) * NW, :], preferred_element_type=jnp.float32
        )
    own_cols = layer_ref[:, pl.ds(pl.multiple_of(f * cd, cd), cd)]
    adapted_ref[...] = (own_cols.astype(jnp.float32) + adapted).astype(jnp.bfloat16)
    squared = jnp.sum(
        jnp.sum(layer_gram * whole_gram, axis=1, keepdims=True), axis=0, keepdims=True
    )
    limit = bound_ref[0]
    norm = jnp.sqrt(squared)
    factor_ref[...] = jnp.broadcast_to(limit / jnp.maximum(norm, limit), factor_ref.shape)
    for copy in sent:
        copy.wait_send()


def grad_kernel(
    RB, layer_ref, up_ref, factor_ref, adapted_in, adapted_ref, clipped_hbm, blocks, sems
):
    factor = factor_ref[0:1, 0:1]
    copies = []
    for i in range(blocks.shape[0]):
        grad = lax.dot_general(
            layer_ref[:, i * RB:(i + 1) * RB], up_ref[...], (((0,), (0,)), ((), ())),
            preferred_element_type=jnp.float32,
        )
        blocks[i] = (grad * factor).astype(jnp.bfloat16)
        copy = pltpu.make_async_copy(
            blocks.at[i], clipped_hbm.at[pl.ds(i * RB, RB), :], sems.at[i]
        )
        copy.start()
        copies.append(copy)
    adapted_ref[...] = adapted_in[...]
    for copy in copies:
        copy.wait()


def per_device(tokens, routes, router, w_gate, w_up, w_down, adapter, upstream, bound):
    E = lax.axis_size("expert")
    F = lax.axis_size("ffn")
    _, tl, D = tokens.shape
    t = routes.shape[1]
    FFD = w_gate.shape[2]
    cd = adapter.shape[2]
    KC = 2 if E * t <= 256 else 4
    NC = max(1, min(4, D // (128 * F)))
    X, T, KW, NW = E // CORES, E * t, D // KC, D // NC
    CW = NW // F
    bf16, f32 = jnp.bfloat16, jnp.float32
    dma = pltpu.SemaphoreType.DMA
    vmem = pl.BlockSpec(memory_space=pltpu.VMEM)
    hbm = pl.BlockSpec(memory_space=pl.ANY)
    scratch = [
        pltpu.VMEM((KC, KW, FFD), bf16),
        pltpu.VMEM((KC, KW, FFD), bf16),
        pltpu.VMEM((NC, FFD, NW), bf16),
        pltpu.VMEM((D, cd), bf16),
        pltpu.VMEM((KC, E, F, tl, KW), bf16),
        pltpu.VMEM((KC, T, KW), bf16),
        pltpu.VMEM((T, FFD), f32),
        pltpu.VMEM((T, FFD), f32),
        pltpu.VMEM((T, FFD), bf16),
        pltpu.VMEM((T, E), f32),
        pltpu.VMEM((E, 2, t), jnp.int32),
        pltpu.VMEM((F, t, t), f32),
        pltpu.VMEM((NC, CORES, X, F, t, CW), bf16),
        pltpu.VMEM((NC, X, F, t, CW), bf16),
        pltpu.VMEM((NC, X, F, t, CW), bf16),
        pltpu.VMEM((NC, X, F, t, CW), bf16),
        pltpu.VMEM((NC, F, t, CW), bf16),
        pltpu.VMEM((NC, F, t, CW), bf16),
        pltpu.VMEM((NC, F, t, CW), bf16),
        dma((4, max(KC, NC))),
        dma((KC + 1,)),
        dma((E,)), dma((E,)),
        dma((F,)), dma((F,)),
        dma((KC, F)), dma((KC, F)),
        dma((KC, X)), dma((KC, X)),
        dma((KC, X)), dma((KC, X)),
        dma((NC,)), dma((NC,)),
        dma((NC, X)), dma((NC, X)),
        dma((NC, F)), dma((NC, F)),
        dma((NC, F)), dma((NC, F)),
    ]
    layer_out, adapted, factor = pl.pallas_call(
        functools.partial(layer_kernel, (E, F, KC, NC, D, FFD, t, tl, cd)),
        out_shape=(
            jax.ShapeDtypeStruct((t, D), bf16),
            jax.ShapeDtypeStruct((t, cd), bf16),
            jax.ShapeDtypeStruct((8, 128), f32),
        ),
        in_specs=[
            vmem, vmem, vmem, hbm, hbm, hbm, hbm, vmem,
            pl.BlockSpec(memory_space=pltpu.SMEM),
        ],
        out_specs=(vmem, vmem, vmem),
        scratch_shapes=scratch,
        compiler_params=pltpu.CompilerParams(
            collective_id=0, has_side_effects=True, vmem_limit_bytes=63_500_000
        ),
    )(
        tokens[0], routes[0].T, router.T, w_gate[0], w_up[0], w_down[0], adapter[0],
        upstream[0], bound,
    )
    RB = D // 8
    adapted, clipped = pl.pallas_call(
        functools.partial(grad_kernel, RB),
        out_shape=(
            jax.ShapeDtypeStruct((t, cd), bf16),
            jax.ShapeDtypeStruct((D, cd), bf16),
        ),
        in_specs=[vmem, vmem, vmem, vmem],
        out_specs=(vmem, hbm),
        scratch_shapes=[pltpu.VMEM((D // RB, RB, cd), bf16), dma((D // RB,))],
    )(layer_out, upstream[0], factor, adapted)
    return (adapted[None], clipped[None])


def solution(mesh):
    in_specs = (
        P("expert", "ffn", None),
        P("expert", None, None),
        P(),
        P("expert", None, "ffn"),
        P("expert", None, "ffn"),
        P("expert", "ffn", None),
        P("expert", None, "ffn"),
        P("expert", None, "ffn"),
        P("expert"),
    )
    out_specs = (P("expert", None, "ffn"), P("expert", None, "ffn"))
    return jax.shard_map(
        per_device, mesh=mesh, in_specs=in_specs, out_specs=out_specs, check_vma=False
    )
```

profile of v0, /device:TPU:2, one launch (start us, length us, event | category | flops | bytes accessed | tf_op | source)
XLA Modules:
  0.0 194.0 jit_solution(2833171252334697976)
XLA Ops:
  1.3 189.4 %shard_map.104 = (bf16[128,4096]{1,0:T(8,128)(2,1)}, bf16[128,128]{1,0:T(8,128)(2,1)}, f32[8,128]{1,0:T(8,128)}) custom-call(bf16[4,4096]{1,0:T(4,128)(2,1)} %bitcast.19, s32[2,128]{1,0:T(2,128)} %bitcast.20, bf16[8,4096]{1,0:T(8,128)(2,1)} %bitcast.18, bf16[4096,384]{1,0:T(8,128)(2,1)} %bitcast.12, bf16[4096,384]{1,0:T(8,128)(2,1)} %bitcast.13, ...), custom_call_target="tpu_custom_call" | custom-call | tf_op jit(solution)/shard_map/pallas_call | solution.py:396
  190.7 3.2 %shard_map.105 = (bf16[128,128]{1,0:T(8,128)(2,1)}, bf16[4096,128]{1,0:T(8,128)(2,1)}) custom-call(bf16[128,4096]{1,0:T(8,128)(2,1)} %get-tuple-element.7.layer_ref, bf16[128,128]{1,0:T(8,128)(2,1)} %bitcast.17, f32[8,128]{1,0:T(8,128)} %get-tuple-element.8.factor_ref, bf16[128,128]{1,0:T(8,128)(2,1)} %get-tuple-element.9.adapted_in), custom_call_target="tpu_custom_call" | custom-call | tf_op jit(solution)/shard_map/pallas_call | solution.py:417
where the time goes:
time: 197 us; the launch traced here: 194 us
  Pallas kernels  193 us (98%)
    pallas_call x1, Pallas kernels, per_device(): pl.pallas_call(functools.partial(layer_kernel, (E, F, KC, NC, D, FFD, t,...  189 us

commit v1 on v0

v1 whole, which is shorter than its diff:
```python
import functools

import jax
import jax.numpy as jnp
from jax import lax
from jax.experimental import pallas as pl
from jax.experimental.pallas import tpu as pltpu
from jax.sharding import PartitionSpec as P

MESH = pl.DeviceIdType.MESH
NZ, NY = 8, 4
CAP = 48
bf16, f32 = jnp.bfloat16, jnp.float32


class Plan:
    def __init__(self, rows, rows_a):
        half_a = -(-rows_a // 32) * 16
        rows_b = rows - rows_a
        half_b = -(-rows_b // 32) * 16
        A = (0, rows_a)
        A1, A2 = (0, half_a), (half_a, rows_a - half_a)
        B = (rows_a, rows_b)
        B1, B2 = (rows_a, half_b), (rows_a + half_b, rows_b - half_b)
        far = NZ // 2
        msgs, deps, gen = {}, {}, {}

        def add(key, step, block, rows, needs):
            msgs[key] = (step, block, rows)
            deps[key] = needs
            gen[key] = 1 + max([gen[n] for n in needs], default=0)

        for k in range(1, far + 1):
            for s in (1, -1):
                rows_k = A if k < far else (A1 if s > 0 else A2)
                add(("Az", s, k), (s, 0), (-s * (k - 1), 0), rows_k,
                    [("Az", s, k - 1)] if k > 1 else [])
        for k in range(1, 3):
            for s in (1, -1):
                rows_k = B if k < 2 else (B1 if s > 0 else B2)
                add(("By", s, k), (0, s), (0, -s * (k - 1)), rows_k,
                    [("By", s, k - 1)] if k > 1 else [])
        for bz in (0, -1, 1, -2, 2, -3, 3, -4):
            if bz == 0:
                needs = []
            elif abs(bz) < far:
                needs = [("Az", 1 if bz < 0 else -1, abs(bz))]
            else:
                needs = [("Az", 1, far), ("Az", -1, far)]
            for k in range(1, 3):
                for s in (1, -1):
                    rows_k = A if k < 2 else (A1 if s > 0 else A2)
                    add(("Ay", bz, s, k), (0, s), (bz, -s * (k - 1)), rows_k,
                        [("Ay", bz, s, k - 1)] if k > 1 else needs)
        for by in (0, -1, 1, 2):
            if by == 0:
                needs = []
            elif abs(by) < 2:
                needs = [("By", 1 if by < 0 else -1, 1)]
            else:
                needs = [("By", 1, 2), ("By", -1, 2)]
            for k in range(1, far + 1):
                for s in (1, -1):
                    rows_k = B if k < far else (B1 if s > 0 else B2)
                    add(("Bz", by, s, k), (s, 0), (-s * (k - 1), by), rows_k,
                        [("Bz", by, s, k - 1)] if k > 1 else needs)
        self.msgs, self.deps, self.gen = msgs, deps, gen
        self.keys = list(msgs)
        self.index = {key: i for i, key in enumerate(self.keys)}
        self.order = sorted(self.keys, key=lambda key: gen[key])
        self.last = max(gen.values())
        self.users = {key: [k2 for k2 in self.keys if key in deps[k2]] for key in self.keys}
        self.offset, total = {}, 0
        for key in self.keys:
            self.offset[key] = total
            total += msgs[key][2][1]
        self.total = total


SLOTS = Plan(8 * CAP, 224)
LAYER = Plan(128, 64)


def layer_kernel(
    tok_ref, routes_ref, router_ref, wg_hbm, wu_hbm, wd_hbm, ad_hbm, up_ref, bound_ref,
    adapted_ref, clipped_ref,
    w, wd, ad, tok_s, tok_y, tok_z, aux_s, aux_y, aux_z, gall, lgp, tcol, pm, whi, wlo,
    pks, buf, acc, hid, vb, rb, rx, lbuf, grad, gram, adp,
    w_sem, a1s, a1r, a2s, a2r, b1s, b1r, b2s, b2r, g1s, g1r, g2s, g2r,
    xs, xr, ys, yr, ags, agr, rss, rsr, lgs, lgr,
):
    E = 8
    D = NZ * NY * 128
    e = lax.axis_index("expert")
    f = lax.axis_index("ffn")
    z, y = f // NY, lax.rem(f, NY)

    loads = []
    for g in range(NZ):
        rows = pl.ds(g * 512, 512)
        loads.append(pltpu.make_async_copy(wg_hbm.at[rows, :], w.at[0, g], w_sem.at[0, g]))
        loads.append(pltpu.make_async_copy(wu_hbm.at[rows, :], w.at[1, g], w_sem.at[1, g]))
    late_loads = []
    for g in range(NZ):
        late_loads.append(pltpu.make_async_copy(
            wd_hbm.at[:, pl.ds(g * 512, 512)], wd.at[g], w_sem.at[2, g]))
        late_loads.append(pltpu.make_async_copy(
            ad_hbm.at[pl.ds(g * 512, 512), :], ad.at[g], w_sem.at[3, g]))

    def at(dz, dy):
        return lax.rem(z + dz + NZ, NZ) * NY + lax.rem(y + dy + NY, NY)

    def ffn(dz, dy):
        return {"ffn": at(dz, dy)}

    def peer(d):
        return {"expert": lax.rem(e + d, E)}

    barrier = pltpu.get_barrier_semaphore()
    for dy in range(1, NY):
        pl.semaphore_signal(barrier, inc=1, device_id=ffn(0, dy), device_id_type=MESH)
    for dz in range(1, NZ):
        pl.semaphore_signal(barrier, inc=1, device_id=ffn(dz, 0), device_id_type=MESH)
    for d in range(1, E):
        pl.semaphore_signal(barrier, inc=1, device_id=peer(d), device_id_type=MESH)

    for load in loads:
        load.start()

    for i in range(NZ * NY):
        tok_s[i % NY, i // NY] = tok_ref[:, i * 128:(i + 1) * 128]
    tok_y[y] = tok_s[y]
    lgp[...] = jnp.zeros_like(lgp)
    lgp[0:4, 0:E] = lax.dot_general(
        tok_ref[...], router_ref[...], (((1,), (1,)), ((), ())), preferred_element_type=f32
    )
    own_logits = lgp[0:4, :]
    own_gram = lax.dot_general(
        up_ref[...], up_ref[...], (((1,), (1,)), ((), ())), preferred_element_type=f32
    )
    for i in range(NZ * NY):
        aux_s[i % NY, i // NY, 0:4, :] = own_logits
        aux_s[i % NY, i // NY, 4:8, :] = own_gram[4 * i:4 * i + 4, :]
    aux_y[y] = aux_s[y]

    first, second = routes_ref[0:1, :], routes_ref[1:2, :]
    expert_ids = lax.broadcasted_iota(jnp.int32, (E, 128), 0)
    hits = ((expert_ids == first) | (expert_ids == second)).astype(f32)
    before = (
        lax.broadcasted_iota(jnp.int32, (128, 128), 0)
        < lax.broadcasted_iota(jnp.int32, (128, 128), 1)
    ).astype(f32)
    rank = jnp.dot(hits.astype(bf16), before.astype(bf16), preferred_element_type=f32)
    slot = jnp.where(hits > 0.0, rank, -1.0)
    slot_ids = lax.broadcasted_iota(jnp.int32, (CAP, 128), 0).astype(f32)
    for i in range(E):
        pm[i * CAP:(i + 1) * CAP, :] = (slot_ids == slot[i:i + 1, :]).astype(f32)

    pl.semaphore_wait(barrier, NY - 1 + NZ - 1 + E - 1)

    sent = []

    def copy_of(src, dst, send_sem, recv_sem, device):
        return pltpu.make_async_remote_copy(
            src_ref=src, dst_ref=dst, send_sem=send_sem, recv_sem=recv_sem,
            device_id=device, device_id_type=MESH,
        )

    def send(src, dst, send_sem, recv_sem, device):
        copy = copy_of(src, dst, send_sem, recv_sem, device)
        copy.start()
        sent.append(copy)

    def receive(dst, send_sem, recv_sem, device):
        copy_of(dst, dst, send_sem, recv_sem, device).wait_recv()

    def col(dy):
        return lax.rem(y + dy + NY, NY)

    def layer_of(dz):
        return lax.rem(z + dz + NZ, NZ)

    for dy in (1, 3, 2):
        send(tok_s.at[col(dy)], tok_y.at[y], a1s.at[dy], a1r.at[dy], ffn(0, dy))
    for dy in (1, 3, 2):
        send(aux_s.at[col(dy)], aux_y.at[y], b1s.at[dy], b1r.at[dy], ffn(0, dy))
    for dy in (1, 3, 2):
        receive(tok_y.at[col(-dy)], a1s.at[dy], a1r.at[dy], ffn(0, dy))
    for dz in (4, 3, 5, 2, 6, 1, 7):
        send(tok_y.at[:, layer_of(dz)], tok_z.at[z], a2s.at[dz], a2r.at[dz], ffn(dz, 0))
    for i in range(NY):
        tok_z[z, i] = tok_y[i, z]
    for dy in (1, 3, 2):
        receive(aux_y.at[col(-dy)], b1s.at[dy], b1r.at[dy], ffn(0, dy))
    for dz in (1, 7, 2, 6, 3, 5, 4):
        receive(tok_z.at[layer_of(-dz)], a2s.at[dz], a2r.at[dz], ffn(dz, 0))
    own_tokens = jnp.concatenate(
        [tok_z[i // NY, i % NY].astype(f32) for i in range(NZ * NY)], axis=0
    ).astype(bf16)
    tcol[...] = own_tokens
    packed = jnp.dot(pm[...].astype(bf16), own_tokens, preferred_element_type=f32).astype(bf16)
    for i in range(E):
        pks[i] = packed[i * CAP:(i + 1) * CAP, :]

    def slot_rows(c):
        return pl.ds(pl.multiple_of(c * CAP, 16), CAP)

    for d in (4, 3, 5, 2, 6, 1, 7):
        send(pks.at[lax.rem(e + d, E)], buf.at[f, slot_rows(e)], xs.at[d], xr.at[d], peer(d))
    buf[f, slot_rows(e), :] = pks[e]
    for dz in range(1, NZ):
        send(aux_y.at[:, layer_of(dz)], aux_z.at[z], b2s.at[dz], b2r.at[dz], ffn(dz, 0))
    for i in range(NY):
        aux_z[z, i] = aux_y[i, z]
    for load in late_loads:
        load.start()
    for d in (1, 7, 2, 6, 3, 5, 4):
        receive(buf.at[f, slot_rows(lax.rem(e + E - d, E))], xs.at[d], xr.at[d], peer(d))

    def gather(plan, ref, send_sems, recv_sems, after):
        done = set()
        started = set()

        def start_ready():
            for key in plan.order:
                if key not in started and all(n in done for n in plan.deps[key]):
                    started.add(key)
                    step, block, (r0, n) = plan.msgs[key]
                    view = ref.at[at(*block), pl.ds(r0, n)]
                    i = plan.index[key]
                    send(view, view, send_sems.at[i], recv_sems.at[i], ffn(*step))

        start_ready()
        for g in range(1, plan.last + 1):
            for key in plan.order:
                if plan.gen[key] == g:
                    step, block, (r0, n) = plan.msgs[key]
                    view = ref.at[at(block[0] - step[0], block[1] - step[1]), pl.ds(r0, n)]
                    i = plan.index[key]
                    receive(view, send_sems.at[i], recv_sems.at[i], ffn(*step))
                    done.add(key)
                    start_ready()
            after(g)

    def aux_part():
        for dz in range(1, NZ):
            receive(aux_z.at[layer_of(-dz)], b2s.at[dz], b2r.at[dz], ffn(dz, 0))
        logit_rows = jnp.concatenate(
            [aux_z[i // NY, i % NY, 0:4, :] for i in range(NZ * NY)], axis=0
        )
        logits = jnp.transpose(logit_rows)[0:E, :]
        total = aux_z[0, 0, 4:8, :]
        for i in range(1, NZ * NY):
            total = total + aux_z[i // NY, i % NY, 4:8, :]
        gall[y, z] = total
        for dz in range(1, NZ):
            send(gall.at[y, z], gall.at[y, z], g1s.at[dz], g1r.at[dz], ffn(dz, 0))
        picked_first = jnp.sum(jnp.where(expert_ids == first, logits, 0.0), axis=0, keepdims=True)
        picked_second = jnp.sum(
            jnp.where(expert_ids == second, logits, 0.0), axis=0, keepdims=True
        )
        weight_first = 1.0 / (1.0 + jnp.exp(picked_second - picked_first))
        weights = jnp.where(expert_ids == first, weight_first, 1.0 - weight_first)
        weighted = jnp.concatenate(
            [pm[i * CAP:(i + 1) * CAP, :] * weights[i:i + 1, :] for i in range(E)], axis=0
        )
        turned = jnp.concatenate(
            [jnp.transpose(weighted[i * 128:(i + 1) * 128, :]) for i in range(E * CAP // 128)],
            axis=1,
        )
        high = turned.astype(bf16)
        whi[...] = high
        wlo[...] = (turned - high.astype(f32)).astype(bf16)

    def gram_part():
        for dz in range(1, NZ):
            receive(gall.at[y, layer_of(-dz)], g1s.at[dz], g1r.at[dz], ffn(dz, 0))
        for dy in range(1, NY):
            send(gall.at[y], gall.at[y], g2s.at[dy], g2r.at[dy], ffn(0, dy))

    groups = {2: (0,), 3: (-1, 1), 4: (-2, 2), 5: (-3, 3), 6: (4,)}

    def expand(g):
        if g == 1:
            aux_part()
            return
        if g == 2:
            for load in loads:
                load.wait()
        if g == 3:
            gram_part()
        for dz in groups[g]:
            zz = layer_of(dz)
            lhs = jnp.concatenate([buf[zz * NY + i] for i in range(NY)], axis=1)
            for m in range(2):
                part = jnp.dot(lhs, w[m, zz], preferred_element_type=f32)
                acc[m] = part if g == 2 else acc[m] + part

    gather(SLOTS, buf, ags, agr, expand)

    gate, up = acc[0], acc[1]
    hid[...] = (gate / (1.0 + jnp.exp(-gate)) * up).astype(bf16)

    for load in late_loads:
        load.wait()
    plan = SLOTS
    got, started, made = set(), set(), set()

    def down(dz):
        zz = layer_of(dz)
        value = jnp.dot(hid[...], wd[zz], preferred_element_type=f32).astype(bf16)
        for i in range(NY):
            vb[zz * NY + i] = value[:, i * 128:(i + 1) * 128]
        made.add(dz % NZ)

    def reduce_ready():
        for key in reversed(plan.order):
            step, block, (r0, n) = plan.msgs[key]
            dest = (block[0] - step[0], block[1] - step[1])
            if (
                key not in started and dest[0] % NZ in made
                and all(u in got for u in plan.users[key])
            ):
                started.add(key)
                i = plan.index[key]
                send(
                    vb.at[at(*dest), pl.ds(r0, n)], rb.at[pl.ds(plan.offset[key], n)],
                    rss.at[i], rsr.at[i], ffn(-step[0], -step[1]),
                )

    for dz in (4, 3, -3, 2, -2, 1, -1, 0):
        down(dz)
        reduce_ready()
    for key in reversed(plan.order):
        step, block, (r0, n) = plan.msgs[key]
        i = plan.index[key]
        rows = pl.ds(plan.offset[key], n)
        receive(rb.at[rows], rss.at[i], rsr.at[i], ffn(-step[0], -step[1]))
        here = at(*block)
        vb[here, r0:r0 + n, :] = (
            vb[here, r0:r0 + n, :].astype(f32) + rb[rows, :].astype(f32)
        ).astype(bf16)
        got.add(key)
        reduce_ready()

    for d in (4, 3, 5, 2, 6, 1, 7):
        send(
            vb.at[f, slot_rows(lax.rem(e + d, E))], rx.at[slot_rows(e)],
            ys.at[d], yr.at[d], peer(d),
        )
    rx[slot_rows(e), :] = vb[f, slot_rows(e), :]
    for dy in range(1, NY):
        receive(gall.at[col(-dy)], g2s.at[dy], g2r.at[dy], ffn(0, dy))
    for d in (1, 7, 2, 6, 3, 5, 4):
        receive(rx.at[slot_rows(lax.rem(e + E - d, E))], ys.at[d], yr.at[d], peer(d))
    mixture = jnp.dot(whi[...], rx[...], preferred_element_type=f32) + jnp.dot(
        wlo[...], rx[...], preferred_element_type=f32
    )
    layer_cols = (tcol[...].astype(f32) + mixture).astype(bf16)
    lbuf[f] = layer_cols

    def contract(g):
        for dz in groups.get(g, ()):
            zz = layer_of(dz)
            block = jnp.concatenate([lbuf[zz * NY + i] for i in range(NY)], axis=1)
            gram_g = lax.dot_general(
                block, block, (((1,), (1,)), ((), ())), preferred_element_type=f32
            )
            adp_g = jnp.dot(block, ad[zz], preferred_element_type=f32)
            gram[...] = gram_g if g == 2 else gram[...] + gram_g
            adp[...] = adp_g if g == 2 else adp[...] + adp_g
            grad[zz] = lax.dot_general(
                block, up_ref[...], (((0,), (0,)), ((), ())), preferred_element_type=f32
            )

    gather(LAYER, lbuf, lgs, lgr, contract)

    whole_gram = jnp.concatenate(
        [gall[i % NY, i // NY] for i in range(NZ * NY)], axis=0
    )
    squared = jnp.sum(
        jnp.sum(gram[...] * whole_gram, axis=1, keepdims=True), axis=0, keepdims=True
    )
    limit = bound_ref[0]
    norm = jnp.sqrt(jnp.maximum(squared, 0.0))
    factor = limit / jnp.maximum(norm, limit)
    adapted_ref[...] = (layer_cols.astype(f32) + adp[...]).astype(bf16)
    for g in range(NZ):
        clipped_ref[g * 512:(g + 1) * 512, :] = (grad[g] * factor).astype(bf16)
    for copy in sent:
        copy.wait_send()


def per_device(tokens, routes, router, w_gate, w_up, w_down, adapter, upstream, bound):
    F, E = NZ * NY, 8
    R = E * CAP
    dma = pltpu.SemaphoreType.DMA
    vmem = pl.BlockSpec(memory_space=pltpu.VMEM)
    hbm = pl.BlockSpec(memory_space=pl.ANY)
    V = pltpu.VMEM
    n1, n2 = len(SLOTS.keys), len(LAYER.keys)
    scratch = [
        V((2, NZ, 512, 384), bf16), V((NZ, 384, 512), bf16), V((NZ, 512, 128), bf16),
        V((NY, NZ, 4, 128), bf16), V((NY, NZ, 4, 128), bf16), V((NZ, NY, 4, 128), bf16),
        V((NY, NZ, 8, 128), f32), V((NY, NZ, 8, 128), f32), V((NZ, NY, 8, 128), f32),
        V((NY, NZ, 4, 128), f32), V((8, 128), f32),
        V((128, 128), bf16), V((R, 128), f32), V((128, R), bf16), V((128, R), bf16),
        V((E, CAP, 128), bf16), V((F, R, 128), bf16), V((2, R, 384), f32), V((R, 384), bf16),
        V((F, R, 128), bf16), V((SLOTS.total, 128), bf16), V((R, 128), bf16),
        V((F, 128, 128), bf16), V((NZ, 512, 128), f32), V((128, 128), f32), V((128, 128), f32),
        dma((4, NZ)),
        dma((NY,)), dma((NY,)), dma((NZ,)), dma((NZ,)),
        dma((NY,)), dma((NY,)), dma((NZ,)), dma((NZ,)),
        dma((NZ,)), dma((NZ,)), dma((NY,)), dma((NY,)),
        dma((E,)), dma((E,)), dma((E,)), dma((E,)),
        dma((n1,)), dma((n1,)), dma((n1,)), dma((n1,)), dma((n2,)), dma((n2,)),
    ]
    adapted, clipped = pl.pallas_call(
        layer_kernel,
        out_shape=(
            jax.ShapeDtypeStruct((128, 128), bf16),
            jax.ShapeDtypeStruct((F * 128, 128), bf16),
        ),
        in_specs=[
            vmem, vmem, vmem, hbm, hbm, hbm, hbm, vmem,
            pl.BlockSpec(memory_space=pltpu.SMEM),
        ],
        out_specs=(vmem, vmem),
        scratch_shapes=scratch,
        compiler_params=pltpu.CompilerParams(
            collective_id=0, has_side_effects=True, vmem_limit_bytes=60_000_000
        ),
    )(
        tokens[0], routes[0].T, router.T, w_gate[0], w_up[0], w_down[0], adapter[0],
        upstream[0], bound,
    )
    return (adapted[None], clipped[None])


def solution(mesh):
    in_specs = (
        P("expert", "ffn", None),
        P("expert", None, None),
        P(),
        P("expert", None, "ffn"),
        P("expert", None, "ffn"),
        P("expert", "ffn", None),
        P("expert", None, "ffn"),
        P("expert", None, "ffn"),
        P("expert"),
    )
    out_specs = (P("expert", None, "ffn"), P("expert", None, "ffn"))
    return jax.shard_map(
        per_device, mesh=mesh, in_specs=in_specs, out_specs=out_specs, check_vma=False
    )
```

time: 197 us -> 113 us (0.57); the launches traced: 194 us -> 112 us
  Pallas kernels: 193 us -> 107 us
  local copies, waits for them, and re-layouts: 0 us -> 3.64 us
    pallas_call x2 -> x1, Pallas kernels: 193 us -> 107 us  [per_device(): pl.pallas_call(layer_kernel, out_shape=(jax.ShapeDtypeStruct((128, 128),...]
    unnamed x0 -> x2, local copies, waits for them, and re-layouts: none -> 3.64 us
where the time goes in v1:
time: 113 us; the launch traced here: 112 us
  Pallas kernels  107 us (95%)
  local copies, waits for them, and re-layouts  3.64 us (3%)
  between operations  1.29 us (1%)
    pallas_call x1, Pallas kernels, per_device(): pl.pallas_call(layer_kernel, out_shape=(jax.ShapeDtypeStruct((128, 128),...  107 us
    unnamed x2, local copies, waits for them, and re-layouts  3.64 us

profile of v1, /device:TPU:2, one launch (start us, length us, event | category | flops | bytes accessed | tf_op | source)
XLA Modules:
  0.0 112.1 jit_solution(12674745306425096276)
XLA Ops:
  1.3 107.1 %shard_map.104 = (bf16[128,128]{1,0:T(8,128)(2,1)}, bf16[4096,128]{1,0:T(8,128)(2,1)}) custom-call(bf16[4,4096]{1,0:T(4,128)(2,1)} %bitcast.18, s32[2,128]{1,0:T(2,128)} %bitcast.21, bf16[8,4096]{1,0:T(8,128)(2,1)} %bitcast.17, bf16[4096,384]{1,0:T(8,128)(2,1)} %bitcast.12, bf16[4096,384]{1,0:T(8,128)(2,1)} %bitcast.13, bf16[384,4096]{1,0:T(8,128)(2,1)} %bitcast.14, ...), custom_call_target="tpu_custom_call" | custom-call | tf_op jit(solution)/shard_map/pallas_call | solution.py:418
  108.4 1.4 %copy.14 = bf16[1,128,128]{2,1,0:T(8,128)(2,1)} copy(bf16[1,128,128]{2,1,0:T(8,128)(2,1)} %bitcast.20) | data formatting | bytes 65536
  109.8 2.3 %copy.15 = bf16[1,4096,128]{2,1,0:T(8,128)(2,1)} copy(bf16[1,4096,128]{2,1,0:T(8,128)(2,1)} %bitcast.15) | data formatting | bytes 2097152

commit v2 on v1

v2 whole, which is shorter than its diff:
```python
import functools

import jax
import jax.numpy as jnp
from jax import lax
from jax.experimental import pallas as pl
from jax.experimental.pallas import tpu as pltpu
from jax.sharding import PartitionSpec as P

MESH = pl.DeviceIdType.MESH
NZ, NY = 8, 4
CAP = 48
bf16, f32 = jnp.bfloat16, jnp.float32


LATENCY, ROUTED, RATE = 2.45, 0.75, 46.6e3
RING, SKIP = {1: 0, 2: 1, 3: 2, 4: 3}, {1: 0, 2: 0, 3: 2, 4: 2}
YRING, YDIRECT = {1: 0, 2: 1}, {1: 0, 2: 0}


class Plan:
    def __init__(self, rows, rows_a, za, ya, yb, zb):
        half_a = -(-rows_a // 32) * 16
        rows_b = rows - rows_a
        half_b = -(-rows_b // 32) * 16
        A = ((0, rows_a), (0, half_a), (half_a, rows_a - half_a))
        B = ((rows_a, rows_b), (rows_a, half_b), (rows_a + half_b, rows_b - half_b))
        self.msgs, self.deps = {}, {}

        def line(name, parents, part, move, needs):
            last = max(parents)
            for k in sorted(parents):
                for s in (1, -1):
                    j = parents[k]
                    rows_k = part[0] if k < last else part[1 if s > 0 else 2]
                    step, block = move(s, k, j)
                    self.msgs[name + (s, k)] = (step, block, rows_k)
                    self.deps[name + (s, k)] = [name + (s, j)] if j else needs

        line(("Az",), za, A, lambda s, k, j: ((s * (k - j), 0), (-s * j, 0)), [])
        line(("By",), yb, B, lambda s, k, j: ((0, s * (k - j)), (0, -s * j)), [])
        for bz in (0, -1, 1, -2, 2, -3, 3, -4):
            needs = [] if bz == 0 else [("Az", -1 if bz > 0 else 1, abs(bz))]
            if abs(bz) == NZ // 2:
                needs = [("Az", 1, NZ // 2), ("Az", -1, NZ // 2)]
            line(("Ay", bz), ya, A, lambda s, k, j: ((0, s * (k - j)), (bz, -s * j)), needs)
        for by in (0, -1, 1, 2):
            needs = [] if by == 0 else [("By", -1 if by > 0 else 1, abs(by))]
            if abs(by) == NY // 2:
                needs = [("By", 1, NY // 2), ("By", -1, NY // 2)]
            line(("Bz", by), zb, B, lambda s, k, j: ((s * (k - j), 0), (-s * j, by)), needs)
        self.keys = list(self.msgs)
        self.index = {key: i for i, key in enumerate(self.keys)}
        self.users = {key: [u for u in self.keys if key in self.deps[u]] for key in self.keys}
        self.offset, self.total = {}, 0
        for key in self.keys:
            self.offset[key] = self.total
            self.total += self.msgs[key][2][1]

    def target(self, key):
        step, block, _ = self.msgs[key]
        return (block[0] - step[0], block[1] - step[1])

    def near(self, dz):
        return (dz + NZ // 2 - 1) % NZ - (NZ // 2 - 1)


def schedule(plan, reduce, costs, extras=()):
    cost_dot, cost_act, cost_down, cost_add = costs
    far_first = (4, 3, -3, 2, -2, 1, -1, 0)

    def shape(key):
        step, _, (_, n) = plan.msgs[key]
        return (step[0] != 0, step[0] + step[1] > 0), abs(step[0] + step[1]), n * 256 / RATE

    def tails(after):
        found = {}

        def tail(key):
            if key not in found:
                _, hops, wire = shape(key)
                found[key] = LATENCY + hops * wire + max([tail(u) for u in after[key]], default=0.0)
            return found[key]

        for key in plan.keys:
            tail(key)
        return found

    tail_of = {"gather": tails(plan.users), "reduce": tails(plan.deps)}
    waits = {"gather": plan.deps, "reduce": plan.users}
    done = {"gather": set(), "reduce": set()}
    started = {"gather": set(), "reduce": set()}
    groups = {dz: {k for k in plan.keys if plan.near(plan.target(k)[0]) == dz} for dz in far_first}
    dots, acted, downs = [], [False], []
    clock, links, flying, steps, extras = [0.0], {}, [], [], list(extras)

    def start_ready():
        ready = [("gather", k) for k in plan.keys if k not in started["gather"]
                 and all(n in done["gather"] for n in plan.deps[k])]
        if reduce:
            ready += [("reduce", k) for k in plan.keys if k not in started["reduce"]
                      and plan.near(plan.target(k)[0]) in downs
                      and all(n in done["reduce"] for n in plan.users[k])]
        ready.sort(key=lambda mk: (-tail_of[mk[0]][mk[1]], plan.index[mk[1]]))
        for mode, key in ready:
            started[mode].add(key)
            link, hops, wire = shape(key)
            if mode == "reduce":
                link = (link[0], not link[1])
            clock[0] += 0.02
            links[link] = max(clock[0], links.get(link, 0.0)) + hops * wire
            flying.append((links[link] + LATENCY + (hops - 1) * ROUTED, len(steps), mode, key))
            steps.append(("send", mode, key))

    start_ready()
    while True:
        flying.sort()
        if flying and flying[0][0] <= clock[0]:
            _, _, mode, key = flying.pop(0)
            clock[0] += 0.02 + (cost_add * plan.msgs[key][2][1] / 112 if mode == "reduce" else 0.0)
            steps.append(("recv", mode, key))
            done[mode].add(key)
            start_ready()
            continue
        full = [dz for dz in reversed(far_first) if dz not in dots and groups[dz] <= done["gather"]]
        if extras and extras[0][1] <= clock[0]:
            name, _, cost = extras.pop(0)
            steps.append(("extra", name, None))
            clock[0] += cost
        elif full:
            dots.append(full[0])
            steps.append(("dot", full[0], len(dots) == 1))
            clock[0] += cost_dot
        elif reduce and len(dots) == NZ and not acted[0]:
            acted[0] = True
            steps.append(("act", None, None))
            clock[0] += cost_act
        elif acted[0] and len(downs) < NZ:
            downs.append(far_first[len(downs)])
            steps.append(("down", downs[-1], None))
            clock[0] += cost_down
            start_ready()
        elif flying:
            clock[0] = max(clock[0], flying[0][0])
        else:
            return steps


SLOTS = Plan(8 * CAP, 224, SKIP, YRING, YDIRECT, RING)
LAYER = Plan(128, 80, SKIP, YDIRECT, YRING, SKIP)
SLOT_STEPS = schedule(
    SLOTS, True, (0.45, 0.2, 0.25, 0.06), (("aux", 1.0, 1.0), ("gram", 7.0, 0.1))
)
LAYER_STEPS = schedule(LAYER, False, (0.15, 0.0, 0.0, 0.0))


def layer_kernel(
    tok_hbm, routes_hbm, router_hbm, wg_hbm, wu_hbm, wd_hbm, ad_hbm, up_hbm, bound_ref,
    layer_hbm, adapted_ref, factor_ref,
    tok_ref, routes_ref, router_ref, up_ref, w, wd, ad, tok_s, tok_y, tok_z, aux_s, aux_y, aux_z, gall, lgp, tcol, pm, whi, wlo,
    pks, buf, acc, hid, vb, rb, rx, lbuf, gram, adp,
    in_sem, out_sem, w_sem, a1s, a1r, a2s, a2r, b1s, b1r, b2s, b2r, g1s, g1r, g2s, g2r,
    xs, xr, ys, yr, ags, agr, rss, rsr, lgs, lgr,
):
    E = 8
    D = NZ * NY * 128
    e = lax.axis_index("expert")
    f = lax.axis_index("ffn")
    z, y = f // NY, lax.rem(f, NY)

    loads = []
    for g in range(NZ):
        rows = pl.ds(g * 512, 512)
        loads.append(pltpu.make_async_copy(wg_hbm.at[rows, :], w.at[0, g], w_sem.at[0, g]))
        loads.append(pltpu.make_async_copy(wu_hbm.at[rows, :], w.at[1, g], w_sem.at[1, g]))
    late_loads = []
    for g in range(NZ):
        late_loads.append(pltpu.make_async_copy(
            wd_hbm.at[:, pl.ds(g * 512, 512)], wd.at[g], w_sem.at[2, g]))
        late_loads.append(pltpu.make_async_copy(
            ad_hbm.at[pl.ds(g * 512, 512), :], ad.at[g], w_sem.at[3, g]))

    def at(dz, dy):
        return lax.rem(z + dz + NZ, NZ) * NY + lax.rem(y + dy + NY, NY)

    def ffn(dz, dy):
        return {"ffn": at(dz, dy)}

    def peer(d):
        return {"expert": lax.rem(e + d, E)}

    barrier = pltpu.get_barrier_semaphore()
    for dy in range(1, NY):
        pl.semaphore_signal(barrier, inc=1, device_id=ffn(0, dy), device_id_type=MESH)
    for dz in range(1, NZ):
        pl.semaphore_signal(barrier, inc=1, device_id=ffn(dz, 0), device_id_type=MESH)
    for d in range(1, E):
        pl.semaphore_signal(barrier, inc=1, device_id=peer(d), device_id_type=MESH)

    small = [
        pltpu.make_async_copy(src, dst, in_sem.at[i])
        for i, (src, dst) in enumerate((
            (tok_hbm, tok_ref), (up_hbm, up_ref), (router_hbm, router_ref),
            (routes_hbm, routes_ref),
        ))
    ]
    for load in small + loads:
        load.start()
    for load in small:
        load.wait()

    for i in range(NZ * NY):
        tok_s[i % NY, i // NY] = tok_ref[:, i * 128:(i + 1) * 128]
    tok_y[y] = tok_s[y]
    lgp[...] = jnp.zeros_like(lgp)
    lgp[0:4, 0:E] = lax.dot_general(
        tok_ref[...], router_ref[...], (((1,), (1,)), ((), ())), preferred_element_type=f32
    )
    own_logits = lgp[0:4, :]
    own_gram = lax.dot_general(
        up_ref[...], up_ref[...], (((1,), (1,)), ((), ())), preferred_element_type=f32
    )
    for i in range(NZ * NY):
        aux_s[i % NY, i // NY, 0:4, :] = own_logits
        aux_s[i % NY, i // NY, 4:8, :] = own_gram[4 * i:4 * i + 4, :]
    aux_y[y] = aux_s[y]

    first, second = routes_ref[0:1, :], routes_ref[1:2, :]
    expert_ids = lax.broadcasted_iota(jnp.int32, (E, 128), 0)
    hits = ((expert_ids == first) | (expert_ids == second)).astype(f32)
    before = (
        lax.broadcasted_iota(jnp.int32, (128, 128), 0)
        < lax.broadcasted_iota(jnp.int32, (128, 128), 1)
    ).astype(f32)
    rank = jnp.dot(hits.astype(bf16), before.astype(bf16), preferred_element_type=f32)
    slot = jnp.where(hits > 0.0, rank, -1.0)
    slot_ids = lax.broadcasted_iota(jnp.int32, (CAP, 128), 0).astype(f32)
    for i in range(E):
        pm[i * CAP:(i + 1) * CAP, :] = (slot_ids == slot[i:i + 1, :]).astype(f32)

    pl.semaphore_wait(barrier, NY - 1 + NZ - 1 + E - 1)

    sent = []

    def copy_of(src, dst, send_sem, recv_sem, device):
        return pltpu.make_async_remote_copy(
            src_ref=src, dst_ref=dst, send_sem=send_sem, recv_sem=recv_sem,
            device_id=device, device_id_type=MESH,
        )

    def send(src, dst, send_sem, recv_sem, device):
        copy = copy_of(src, dst, send_sem, recv_sem, device)
        copy.start()
        sent.append(copy)

    def receive(dst, send_sem, recv_sem, device):
        copy_of(dst, dst, send_sem, recv_sem, device).wait_recv()

    def col(dy):
        return lax.rem(y + dy + NY, NY)

    def layer_of(dz):
        return lax.rem(z + dz + NZ, NZ)

    for dy in (1, 3, 2):
        send(tok_s.at[col(dy)], tok_y.at[y], a1s.at[dy], a1r.at[dy], ffn(0, dy))
    for dy in (1, 3, 2):
        send(aux_s.at[col(dy)], aux_y.at[y], b1s.at[dy], b1r.at[dy], ffn(0, dy))
    for dy in (1, 3, 2):
        receive(tok_y.at[col(-dy)], a1s.at[dy], a1r.at[dy], ffn(0, dy))
    for dz in (4, 3, 5, 2, 6, 1, 7):
        send(tok_y.at[:, layer_of(dz)], tok_z.at[z], a2s.at[dz], a2r.at[dz], ffn(dz, 0))
    for i in range(NY):
        tok_z[z, i] = tok_y[i, z]
    for dy in (1, 3, 2):
        receive(aux_y.at[col(-dy)], b1s.at[dy], b1r.at[dy], ffn(0, dy))
    for dz in (1, 7, 2, 6, 3, 5, 4):
        receive(tok_z.at[layer_of(-dz)], a2s.at[dz], a2r.at[dz], ffn(dz, 0))
    own_tokens = jnp.concatenate(
        [tok_z[i // NY, i % NY].astype(f32) for i in range(NZ * NY)], axis=0
    ).astype(bf16)
    tcol[...] = own_tokens
    packed = jnp.dot(pm[...].astype(bf16), own_tokens, preferred_element_type=f32).astype(bf16)
    for i in range(E):
        pks[i] = packed[i * CAP:(i + 1) * CAP, :]

    def slot_rows(c):
        return pl.ds(pl.multiple_of(c * CAP, 16), CAP)

    for d in (4, 3, 5, 2, 6, 1, 7):
        send(pks.at[lax.rem(e + d, E)], buf.at[f, slot_rows(e)], xs.at[d], xr.at[d], peer(d))
    buf[f, slot_rows(e), :] = pks[e]
    for dz in range(1, NZ):
        send(aux_y.at[:, layer_of(dz)], aux_z.at[z], b2s.at[dz], b2r.at[dz], ffn(dz, 0))
    for i in range(NY):
        aux_z[z, i] = aux_y[i, z]
    for load in late_loads:
        load.start()
    for d in (1, 7, 2, 6, 3, 5, 4):
        receive(buf.at[f, slot_rows(lax.rem(e + E - d, E))], xs.at[d], xr.at[d], peer(d))

    def aux_part():
        for dz in range(1, NZ):
            receive(aux_z.at[layer_of(-dz)], b2s.at[dz], b2r.at[dz], ffn(dz, 0))
        logit_rows = jnp.concatenate(
            [aux_z[i // NY, i % NY, 0:4, :] for i in range(NZ * NY)], axis=0
        )
        logits = jnp.transpose(logit_rows)[0:E, :]
        total = aux_z[0, 0, 4:8, :]
        for i in range(1, NZ * NY):
            total = total + aux_z[i // NY, i % NY, 4:8, :]
        gall[y, z] = total
        for dz in range(1, NZ):
            send(gall.at[y, z], gall.at[y, z], g1s.at[dz], g1r.at[dz], ffn(dz, 0))
        picked_first = jnp.sum(jnp.where(expert_ids == first, logits, 0.0), axis=0, keepdims=True)
        picked_second = jnp.sum(
            jnp.where(expert_ids == second, logits, 0.0), axis=0, keepdims=True
        )
        weight_first = 1.0 / (1.0 + jnp.exp(picked_second - picked_first))
        weights = jnp.where(expert_ids == first, weight_first, 1.0 - weight_first)
        weighted = jnp.concatenate(
            [pm[i * CAP:(i + 1) * CAP, :] * weights[i:i + 1, :] for i in range(E)], axis=0
        )
        turned = jnp.concatenate(
            [jnp.transpose(weighted[i * 128:(i + 1) * 128, :]) for i in range(E * CAP // 128)],
            axis=1,
        )
        high = turned.astype(bf16)
        whi[...] = high
        wlo[...] = (turned - high.astype(f32)).astype(bf16)

    def gram_part():
        for dz in range(1, NZ):
            receive(gall.at[y, layer_of(-dz)], g1s.at[dz], g1r.at[dz], ffn(dz, 0))
        for dy in range(1, NY):
            send(gall.at[y], gall.at[y], g2s.at[dy], g2r.at[dy], ffn(0, dy))

    def gather_send(plan, ref, sems, key):
        step, block, (r0, n) = plan.msgs[key]
        view = ref.at[at(*block), pl.ds(r0, n)]
        i = plan.index[key]
        send(view, view, sems[0].at[i], sems[1].at[i], ffn(*step))

    def gather_receive(plan, ref, sems, key):
        step, _, (r0, n) = plan.msgs[key]
        view = ref.at[at(*plan.target(key)), pl.ds(r0, n)]
        i = plan.index[key]
        receive(view, sems[0].at[i], sems[1].at[i], ffn(*step))

    def reduce_send(plan, key):
        step, _, (r0, n) = plan.msgs[key]
        i = plan.index[key]
        send(
            vb.at[at(*plan.target(key)), pl.ds(r0, n)], rb.at[pl.ds(plan.offset[key], n)],
            rss.at[i], rsr.at[i], ffn(-step[0], -step[1]),
        )

    def reduce_receive(plan, key):
        step, block, (r0, n) = plan.msgs[key]
        i = plan.index[key]
        rows = pl.ds(plan.offset[key], n)
        receive(rb.at[rows], rss.at[i], rsr.at[i], ffn(-step[0], -step[1]))
        here = at(*block)
        vb[here, r0:r0 + n, :] = (
            vb[here, r0:r0 + n, :].astype(f32) + rb[rows, :].astype(f32)
        ).astype(bf16)

    def expand(dz, opening):
        if opening:
            for load in loads:
                load.wait()
        zz = layer_of(dz)
        lhs = jnp.concatenate([buf[zz * NY + i] for i in range(NY)], axis=1)
        for m in range(2):
            part = jnp.dot(lhs, w[m, zz], preferred_element_type=f32)
            acc[m] = part if opening else acc[m] + part

    def activate():
        gate, up = acc[0], acc[1]
        hid[...] = (gate / (1.0 + jnp.exp(-gate)) * up).astype(bf16)
        for load in late_loads:
            load.wait()

    def down(dz):
        zz = layer_of(dz)
        value = jnp.dot(hid[...], wd[zz], preferred_element_type=f32).astype(bf16)
        for i in range(NY):
            vb[zz * NY + i] = value[:, i * 128:(i + 1) * 128]

    for kind, first_arg, second_arg in SLOT_STEPS:
        if kind == "send" and first_arg == "gather":
            gather_send(SLOTS, buf, (ags, agr), second_arg)
        elif kind == "recv" and first_arg == "gather":
            gather_receive(SLOTS, buf, (ags, agr), second_arg)
        elif kind == "send":
            reduce_send(SLOTS, second_arg)
        elif kind == "recv":
            reduce_receive(SLOTS, second_arg)
        elif kind == "dot":
            expand(first_arg, second_arg)
        elif kind == "act":
            activate()
        elif kind == "down":
            down(first_arg)
        elif first_arg == "aux":
            aux_part()
        else:
            gram_part()

    for d in (4, 3, 5, 2, 6, 1, 7):
        send(
            vb.at[f, slot_rows(lax.rem(e + d, E))], rx.at[slot_rows(e)],
            ys.at[d], yr.at[d], peer(d),
        )
    rx[slot_rows(e), :] = vb[f, slot_rows(e), :]
    for dy in range(1, NY):
        receive(gall.at[col(-dy)], g2s.at[dy], g2r.at[dy], ffn(0, dy))
    for d in (1, 7, 2, 6, 3, 5, 4):
        receive(rx.at[slot_rows(lax.rem(e + E - d, E))], ys.at[d], yr.at[d], peer(d))
    mixture = jnp.dot(whi[...], rx[...], preferred_element_type=f32) + jnp.dot(
        wlo[...], rx[...], preferred_element_type=f32
    )
    layer_cols = tcol[...].astype(f32) + mixture
    lbuf[f] = jnp.transpose(layer_cols).astype(bf16)
    outs = []

    def contract(dz, opening):
        zz = layer_of(dz)
        blocks = pl.ds(zz * NY, NY)
        out = pltpu.make_async_copy(lbuf.at[blocks], layer_hbm.at[blocks], out_sem.at[len(outs)])
        out.start()
        outs.append(out)
        block = jnp.concatenate([lbuf[zz * NY + i] for i in range(NY)], axis=0)
        turned = (((0,), (0,)), ((), ()))
        gram_g = lax.dot_general(block, block, turned, preferred_element_type=f32)
        adp_g = lax.dot_general(block, ad[zz], turned, preferred_element_type=f32)
        gram[...] = gram_g if opening else gram[...] + gram_g
        adp[...] = adp_g if opening else adp[...] + adp_g

    for kind, first_arg, second_arg in LAYER_STEPS:
        if kind == "send":
            gather_send(LAYER, lbuf, (lgs, lgr), second_arg)
        elif kind == "recv":
            gather_receive(LAYER, lbuf, (lgs, lgr), second_arg)
        else:
            contract(first_arg, second_arg)

    whole_gram = jnp.concatenate(
        [gall[i % NY, i // NY] for i in range(NZ * NY)], axis=0
    )
    squared = jnp.sum(
        jnp.sum(gram[...] * whole_gram, axis=1, keepdims=True), axis=0, keepdims=True
    )
    limit = bound_ref[0]
    norm = jnp.sqrt(jnp.maximum(squared, 0.0))
    factor_ref[...] = jnp.broadcast_to(limit / jnp.maximum(norm, limit), factor_ref.shape)
    own_cols = layer_cols.astype(bf16).astype(f32)
    adapted_ref[...] = (own_cols + adp[...]).astype(bf16)
    for copy in sent:
        copy.wait_send()
    for out in outs:
        out.wait()


def grad_kernel(
    layer_hbm, up_hbm, factor_hbm, adapted_hbm, adapted_out, clipped_hbm,
    layer, up, factor, adapted, blocks, in_sem, small_sem, out_sem,
):
    small = [
        pltpu.make_async_copy(src, dst, small_sem.at[i])
        for i, (src, dst) in enumerate((
            (up_hbm, up), (factor_hbm, factor), (adapted_hbm, adapted),
        ))
    ]
    loads = [
        pltpu.make_async_copy(layer_hbm.at[pl.ds(g * NY, NY)], layer.at[g], in_sem.at[g])
        for g in range(NZ)
    ]
    for load in small + loads:
        load.start()
    for load in small:
        load.wait()
    last = pltpu.make_async_copy(adapted, adapted_out, small_sem.at[3])
    last.start()
    stores = []
    scale = factor[0:1, 0:1]
    for g in range(NZ):
        loads[g].wait()
        part = jnp.concatenate([layer[g, i] for i in range(NY)], axis=0)
        grad = jnp.dot(part, up[...], preferred_element_type=f32)
        blocks[g] = (grad * scale).astype(bf16)
        store = pltpu.make_async_copy(
            blocks.at[g], clipped_hbm.at[pl.ds(g * 512, 512), :], out_sem.at[g]
        )
        store.start()
        stores.append(store)
    last.wait()
    for store in stores:
        store.wait()


def per_device(tokens, routes, router, w_gate, w_up, w_down, adapter, upstream, bound):
    F, E = NZ * NY, 8
    R = E * CAP
    dma = pltpu.SemaphoreType.DMA
    vmem = pl.BlockSpec(memory_space=pltpu.VMEM)
    hbm = pl.BlockSpec(memory_space=pl.ANY)
    V = pltpu.VMEM
    n1, n2 = len(SLOTS.keys), len(LAYER.keys)
    scratch = [
        V((4, NZ * NY * 128), bf16), V((2, 128), jnp.int32), V((E, NZ * NY * 128), bf16),
        V((128, 128), bf16),
        V((2, NZ, 512, 384), bf16), V((NZ, 384, 512), bf16), V((NZ, 512, 128), bf16),
        V((NY, NZ, 4, 128), bf16), V((NY, NZ, 4, 128), bf16), V((NZ, NY, 4, 128), bf16),
        V((NY, NZ, 8, 128), f32), V((NY, NZ, 8, 128), f32), V((NZ, NY, 8, 128), f32),
        V((NY, NZ, 4, 128), f32), V((8, 128), f32),
        V((128, 128), bf16), V((R, 128), f32), V((128, R), bf16), V((128, R), bf16),
        V((E, CAP, 128), bf16), V((F, R, 128), bf16), V((2, R, 384), f32), V((R, 384), bf16),
        V((F, R, 128), bf16), V((SLOTS.total, 128), bf16), V((R, 128), bf16),
        V((F, 128, 128), bf16), V((128, 128), f32), V((128, 128), f32),
        dma((4,)), dma((NZ,)), dma((4, NZ)),
        dma((NY,)), dma((NY,)), dma((NZ,)), dma((NZ,)),
        dma((NY,)), dma((NY,)), dma((NZ,)), dma((NZ,)),
        dma((NZ,)), dma((NZ,)), dma((NY,)), dma((NY,)),
        dma((E,)), dma((E,)), dma((E,)), dma((E,)),
        dma((n1,)), dma((n1,)), dma((n1,)), dma((n1,)), dma((n2,)), dma((n2,)),
    ]
    layer, adapted, factor = pl.pallas_call(
        layer_kernel,
        out_shape=(
            jax.ShapeDtypeStruct((F, 128, 128), bf16),
            jax.ShapeDtypeStruct((128, 128), bf16),
            jax.ShapeDtypeStruct((8, 128), f32),
        ),
        in_specs=[hbm] * 8 + [pl.BlockSpec(memory_space=pltpu.SMEM)],
        out_specs=(hbm, vmem, vmem),
        scratch_shapes=scratch,
        compiler_params=pltpu.CompilerParams(
            collective_id=0, has_side_effects=True, vmem_limit_bytes=60_000_000
        ),
    )(
        tokens[0], routes[0].T, router.T, w_gate[0], w_up[0], w_down[0], adapter[0],
        upstream[0], bound,
    )
    adapted, clipped = pl.pallas_call(
        grad_kernel,
        out_shape=(
            jax.ShapeDtypeStruct((128, 128), bf16),
            jax.ShapeDtypeStruct((F * 128, 128), bf16),
        ),
        in_specs=[hbm] * 4,
        out_specs=(hbm, hbm),
        scratch_shapes=[
            V((NZ, NY, 128, 128), bf16), V((128, 128), bf16), V((8, 128), f32),
            V((128, 128), bf16), V((NZ, 512, 128), bf16),
            dma((NZ,)), dma((4,)), dma((NZ,)),
        ],
    )(layer, upstream[0], factor, adapted)
    return (adapted[None], clipped[None])


def solution(mesh):
    in_specs = (
        P("expert", "ffn", None),
        P("expert", None, None),
        P(),
        P("expert", None, "ffn"),
        P("expert", None, "ffn"),
        P("expert", "ffn", None),
        P("expert", None, "ffn"),
        P("expert", None, "ffn"),
        P("expert"),
    )
    out_specs = (P("expert", None, "ffn"), P("expert", None, "ffn"))
    return jax.shard_map(
        per_device, mesh=mesh, in_specs=in_specs, out_specs=out_specs, check_vma=False
    )
```

time: 113 us -> 97.8 us (0.87)
  Pallas kernels: 107 us -> 96.4 us
  local copies, waits for them, and re-layouts: 3.64 us -> 0 us
    pallas_call x1 -> x2, Pallas kernels: 107 us -> 96.4 us  [the longest x1 92.8 us: per_device(): pl.pallas_call(layer_kernel, out_shape=(jax.ShapeDtypeStruct((F, 128, 128...]
    unnamed x2 -> x0, local copies, waits for them, and re-layouts: 3.64 us -> none
where the time goes in v2:
time: 97.8 us; the launch traced here: 97.6 us
  Pallas kernels  96.4 us (99%)
  between operations  1.29 us (1%)
    pallas_call x1, Pallas kernels, per_device(): pl.pallas_call(layer_kernel, out_shape=(jax.ShapeDtypeStruct((F, 128, 128...  92.8 us
    pallas_call x1, Pallas kernels, per_device(): pl.pallas_call(grad_kernel, out_shape=(jax.ShapeDtypeStruct((128, 128), b...  3.6 us

profile of v2, /device:TPU:2, one launch (start us, length us, event | category | flops | bytes accessed | tf_op | source)
XLA Modules:
  0.0 97.6 jit_solution(792658913912239124)
XLA Ops:
  1.3 92.8 %shard_map.104 = (bf16[32,128,128]{2,1,0:T(8,128)(2,1)}, bf16[128,128]{1,0:T(8,128)(2,1)}, f32[8,128]{1,0:T(8,128)}) custom-call(bf16[4,4096]{1,0:T(4,128)(2,1)} %bitcast.19, s32[2,128]{1,0:T(2,128)} %bitcast.20, bf16[8,4096]{1,0:T(8,128)(2,1)} %bitcast.18, bf16[4096,384]{1,0:T(8,128)(2,1)} %bitcast.12, bf16[4096,384]{1,0:T(8,128)(2,1)} %bitcast.13, ...), custom_call_target="tpu_custom_call" | custom-call | tf_op jit(solution)/shard_map/pallas_call | solution.py:528
  94.0 3.6 %shard_map.105 = (bf16[128,128]{1,0:T(8,128)(2,1)}, bf16[4096,128]{1,0:T(8,128)(2,1)}) custom-call(bf16[32,128,128]{2,1,0:T(8,128)(2,1)} %get-tuple-element.7.layer_hbm, bf16[128,128]{1,0:T(8,128)(2,1)} %bitcast.17, f32[8,128]{1,0:T(8,128)} %get-tuple-element.8.factor_hbm, bf16[128,128]{1,0:T(8,128)(2,1)} %get-tuple-element.9.adapted_hbm), custom_call_target="tpu_custom_call" | custom-call | tf_op jit(solution)/shard_map/pallas_call | solution.py:545

commit v3 on v2

--- a/solution.py
+++ b/solution.py
@@ -462,31 +462,13 @@
         out.wait()
 
 
-def grad_kernel(
-    layer_hbm, up_hbm, factor_hbm, adapted_hbm, adapted_out, clipped_hbm,
-    layer, up, factor, adapted, blocks, in_sem, small_sem, out_sem,
-):
-    small = [
-        pltpu.make_async_copy(src, dst, small_sem.at[i])
-        for i, (src, dst) in enumerate((
-            (up_hbm, up), (factor_hbm, factor), (adapted_hbm, adapted),
-        ))
-    ]
-    loads = [
-        pltpu.make_async_copy(layer_hbm.at[pl.ds(g * NY, NY)], layer.at[g], in_sem.at[g])
-        for g in range(NZ)
-    ]
-    for load in small + loads:
-        load.start()
-    for load in small:
-        load.wait()
-    last = pltpu.make_async_copy(adapted, adapted_out, small_sem.at[3])
+def grad_kernel(layer, up, factor, adapted, adapted_out, clipped_hbm, blocks, last_sem, out_sem):
+    last = pltpu.make_async_copy(adapted, adapted_out, last_sem)
     last.start()
     stores = []
     scale = factor[0:1, 0:1]
     for g in range(NZ):
-        loads[g].wait()
-        part = jnp.concatenate([layer[g, i] for i in range(NY)], axis=0)
+        part = jnp.concatenate([layer[g * NY + i] for i in range(NY)], axis=0)
         grad = jnp.dot(part, up[...], preferred_element_type=f32)
         blocks[g] = (grad * scale).astype(bf16)
         store = pltpu.make_async_copy(
@@ -536,11 +518,14 @@
         out_specs=(hbm, vmem, vmem),
         scratch_shapes=scratch,
         compiler_params=pltpu.CompilerParams(
-            collective_id=0, has_side_effects=True, vmem_limit_bytes=60_000_000
+            collective_id=0, has_side_effects=True, vmem_limit_bytes=55_000_000
         ),
     )(
-        tokens[0], routes[0].T, router.T, w_gate[0], w_up[0], w_down[0], adapter[0],
-        upstream[0], bound,
+        *[pltpu.with_memory_space_constraint(a, pltpu.HBM) for a in (
+            tokens[0], routes[0].T, router.T, w_gate[0], w_up[0], w_down[0], adapter[0],
+            upstream[0],
+        )],
+        bound,
     )
     adapted, clipped = pl.pallas_call(
         grad_kernel,
@@ -548,13 +533,12 @@
             jax.ShapeDtypeStruct((128, 128), bf16),
             jax.ShapeDtypeStruct((F * 128, 128), bf16),
         ),
-        in_specs=[hbm] * 4,
+        in_specs=[vmem] * 4,
         out_specs=(hbm, hbm),
         scratch_shapes=[
-            V((NZ, NY, 128, 128), bf16), V((128, 128), bf16), V((8, 128), f32),
-            V((128, 128), bf16), V((NZ, 512, 128), bf16),
-            dma((NZ,)), dma((4,)), dma((NZ,)),
+            V((NZ, 512, 128), bf16), pltpu.SemaphoreType.DMA, dma((NZ,)),
         ],
+        compiler_params=pltpu.CompilerParams(vmem_limit_bytes=8_000_000),
     )(layer, upstream[0], factor, adapted)
     return (adapted[None], clipped[None])
 

time: 97.8 us -> 95.7 us (0.979)
  Pallas kernels: 96.4 us -> 94.3 us
    pallas_call x1, Pallas kernels: 3.6 us -> 1.25 us  [per_device(): pl.pallas_call(grad_kernel, out_shape=(jax.ShapeDtypeStruct((128, 128), b...]
where the time goes in v3:
time: 95.7 us; the launch traced here: 95.6 us
  Pallas kernels  94.3 us (99%)
  between operations  1.3 us (1%)
    pallas_call x1, Pallas kernels, per_device(): pl.pallas_call(layer_kernel, out_shape=(jax.ShapeDtypeStruct((F, 128, 128...  93 us

profile of v3, /device:TPU:2, one launch (start us, length us, event | category | flops | bytes accessed | tf_op | source)
XLA Modules:
  0.0 95.6 jit_solution(5305772122020724441)
XLA Ops:
  1.3 0.0 copy-start
  1.3 93.0 %shard_map.104 = (bf16[32,128,128]{2,1,0:T(8,128)(2,1)S(1)}, bf16[128,128]{1,0:T(8,128)(2,1)S(1)}, f32[8,128]{1,0:T(8,128)S(1)}) custom-call(bf16[4,4096]{1,0:T(4,128)(2,1)} %bitcast.19, s32[2,128]{1,0:T(2,128)} %bitcast.20, bf16[8,4096]{1,0:T(8,128)(2,1)} %bitcast.18, bf16[4096,384]{1,0:T(8,128)(2,1)} %bitcast.14, bf16[4096,384]{1,0:T(8,128)(2,1)} %bitcast.15, ...), custom_call_target="tpu_custom_call" | custom-call | tf_op jit(solution)/shard_map/pallas_call | solution.py:510
  94.3 0.0 copy-done
  94.3 1.2 %shard_map.105 = (bf16[128,128]{1,0:T(8,128)(2,1)}, bf16[4096,128]{1,0:T(8,128)(2,1)}) custom-call(bf16[32,128,128]{2,1,0:T(8,128)(2,1)S(1)} %get-tuple-element.7.layer, bf16[128,128]{1,0:T(8,128)(2,1)S(1)} %bitcast.13, f32[8,128]{1,0:T(8,128)S(1)} %get-tuple-element.8.factor, bf16[128,128]{1,0:T(8,128)(2,1)S(1)} %get-tuple-element.9.adapted), custom_call_target="tpu_custom_call" | custom-call | tf_op jit(solution)/shard_map/pallas_call | solution.py:530
Async XLA Ops:
  1.3 93.0 %copy-start = (bf16[1,128,128]{2,1,0:T(8,128)(2,1)S(1)}, bf16[1,128,128]{2,1,0:T(8,128)(2,1)}, u32[]{:S(2)}) copy-start(bf16[1,128,128]{2,1,0:T(8,128)(2,1)} %param.16) | copy-start | bytes 98308

commit v4 on v3

--- a/solution.py
+++ b/solution.py
@@ -13,13 +13,14 @@
 bf16, f32 = jnp.bfloat16, jnp.float32
 
 
-LATENCY, ROUTED, RATE = 2.45, 0.75, 46.6e3
+LATENCY, ROUTED, RATE = 2.0, 0.75, 46.6e3
 RING, SKIP = {1: 0, 2: 1, 3: 2, 4: 3}, {1: 0, 2: 0, 3: 2, 4: 2}
+HALFSKIP = {1: 0, 2: 0, 3: 2, 4: 3}
 YRING, YDIRECT = {1: 0, 2: 1}, {1: 0, 2: 0}
 
 
 class Plan:
-    def __init__(self, rows, rows_a, za, ya, yb, zb):
+    def __init__(self, base, rows, rows_a, za, ya, yb, zb):
         half_a = -(-rows_a // 32) * 16
         rows_b = rows - rows_a
         half_b = -(-rows_b // 32) * 16
@@ -33,8 +34,10 @@
                 for s in (1, -1):
                     j = parents[k]
                     rows_k = part[0] if k < last else part[1 if s > 0 else 2]
+                    if rows_k[1] == 0:
+                        continue
                     step, block = move(s, k, j)
-                    self.msgs[name + (s, k)] = (step, block, rows_k)
+                    self.msgs[name + (s, k)] = (step, block, (base + rows_k[0], rows_k[1]))
                     self.deps[name + (s, k)] = [name + (s, j)] if j else needs
 
         line(("Az",), za, A, lambda s, k, j: ((s * (k - j), 0), (-s * j, 0)), [])
@@ -65,100 +68,119 @@
         return (dz + NZ // 2 - 1) % NZ - (NZ // 2 - 1)
 
 
-def schedule(plan, reduce, costs, extras=()):
+def schedule(plans, starts, reduce, costs, throttle, extras=()):
     cost_dot, cost_act, cost_down, cost_add = costs
     far_first = (4, 3, -3, 2, -2, 1, -1, 0)
-
-    def shape(key):
-        step, _, (_, n) = plan.msgs[key]
-        return (step[0] != 0, step[0] + step[1] > 0), abs(step[0] + step[1]), n * 256 / RATE
+    keys = [(h, key) for h, plan in enumerate(plans) for key in plan.keys]
+    place = {hk: i for i, hk in enumerate(keys)}
+    deps = {(h, k): [(h, n) for n in plans[h].deps[k]] for h, k in keys}
+    users = {(h, k): [(h, n) for n in plans[h].users[k]] for h, k in keys}
+    goal = {(h, k): plans[h].near(plans[h].target(k)[0]) for h, k in keys}
+
+    def shape(hk):
+        step, _, (_, n) = plans[hk[0]].msgs[hk[1]]
+        return (step[0] != 0, step[0] + step[1] > 0), abs(step[0] + step[1]), 0.03 + n * 256 / RATE
 
     def tails(after):
         found = {}
 
-        def tail(key):
-            if key not in found:
-                _, hops, wire = shape(key)
-                found[key] = LATENCY + hops * wire + max([tail(u) for u in after[key]], default=0.0)
-            return found[key]
-
-        for key in plan.keys:
-            tail(key)
+        def tail(hk):
+            if hk not in found:
+                _, hops, wire = shape(hk)
+                found[hk] = LATENCY + hops * wire + max([tail(u) for u in after[hk]], default=0.0)
+            return found[hk]
+
+        for hk in keys:
+            tail(hk)
         return found
 
-    tail_of = {"gather": tails(plan.users), "reduce": tails(plan.deps)}
-    waits = {"gather": plan.deps, "reduce": plan.users}
+    tail_of = {"gather": tails(users), "reduce": tails(deps)}
+    before = {"gather": deps, "reduce": users}
     done = {"gather": set(), "reduce": set()}
-    started = {"gather": set(), "reduce": set()}
-    groups = {dz: {k for k in plan.keys if plan.near(plan.target(k)[0]) == dz} for dz in far_first}
-    dots, acted, downs = [], [False], []
-    clock, links, flying, steps, extras = [0.0], {}, [], [], list(extras)
-
-    def start_ready():
-        ready = [("gather", k) for k in plan.keys if k not in started["gather"]
-                 and all(n in done["gather"] for n in plan.deps[k])]
-        if reduce:
-            ready += [("reduce", k) for k in plan.keys if k not in started["reduce"]
-                      and plan.near(plan.target(k)[0]) in downs
-                      and all(n in done["reduce"] for n in plan.users[k])]
-        ready.sort(key=lambda mk: (-tail_of[mk[0]][mk[1]], plan.index[mk[1]]))
-        for mode, key in ready:
-            started[mode].add(key)
-            link, hops, wire = shape(key)
+    queued = {"gather": set(), "reduce": set()}
+    groups = {dz: {hk for hk in keys if goal[hk] == dz} for dz in far_first}
+    dots, acted, downs, ended = [], False, [], set()
+    clock, links, flying, steps, extras, ready = 0.0, {}, [], [], list(extras), []
+    while True:
+        for mode in ("gather", "reduce"):
+            for hk in keys:
+                if hk not in queued[mode] and all(n in done[mode] for n in before[mode][hk]) and (
+                    clock >= starts[hk[0]] if mode == "gather" else goal[hk] in downs
+                ):
+                    queued[mode].add(hk)
+                    rank = tail_of[mode][hk] + (100.0 if mode == "gather" else 0.0)
+                    ready.append((-rank, place[hk], mode, hk))
+        ready.sort()
+        for item in list(ready):
+            _, _, mode, hk = item
+            link, hops, wire = shape(hk)
             if mode == "reduce":
                 link = (link[0], not link[1])
-            clock[0] += 0.02
-            links[link] = max(clock[0], links.get(link, 0.0)) + hops * wire
-            flying.append((links[link] + LATENCY + (hops - 1) * ROUTED, len(steps), mode, key))
-            steps.append(("send", mode, key))
-
-    start_ready()
-    while True:
+            if links.get(link, 0.0) - clock < throttle:
+                ready.remove(item)
+                clock += 0.035
+                links[link] = max(clock, links.get(link, 0.0)) + hops * wire
+                flying.append((links[link] + LATENCY + (hops - 1) * ROUTED, len(steps), mode, hk))
+                steps.append(("send", mode, hk))
         flying.sort()
-        if flying and flying[0][0] <= clock[0]:
-            _, _, mode, key = flying.pop(0)
-            clock[0] += 0.02 + (cost_add * plan.msgs[key][2][1] / 112 if mode == "reduce" else 0.0)
-            steps.append(("recv", mode, key))
-            done[mode].add(key)
-            start_ready()
+        if flying and flying[0][0] <= clock:
+            _, _, mode, hk = flying.pop(0)
+            clock += 0.035
+            if mode == "reduce":
+                clock += cost_add * shape(hk)[2]
+            steps.append(("recv", mode, hk))
+            done[mode].add(hk)
+            h = hk[0]
+            if mode == "reduce" and h not in ended and all(
+                (h, k) in done["reduce"] for k in plans[h].keys
+            ):
+                ended.add(h)
+                steps.append(("end", h, None))
             continue
         full = [dz for dz in reversed(far_first) if dz not in dots and groups[dz] <= done["gather"]]
-        if extras and extras[0][1] <= clock[0]:
+        waiting = [start for start in starts if start > clock]
+        if extras and extras[0][1] <= clock:
             name, _, cost = extras.pop(0)
             steps.append(("extra", name, None))
-            clock[0] += cost
+            clock += cost
         elif full:
             dots.append(full[0])
             steps.append(("dot", full[0], len(dots) == 1))
-            clock[0] += cost_dot
-        elif reduce and len(dots) == NZ and not acted[0]:
-            acted[0] = True
+            clock += cost_dot
+        elif reduce and len(dots) == NZ and not acted:
+            acted = True
             steps.append(("act", None, None))
-            clock[0] += cost_act
-        elif acted[0] and len(downs) < NZ:
+            clock += cost_act
+        elif acted and len(downs) < NZ:
             downs.append(far_first[len(downs)])
             steps.append(("down", downs[-1], None))
-            clock[0] += cost_down
-            start_ready()
-        elif flying:
-            clock[0] = max(clock[0], flying[0][0])
+            clock += cost_down
+        elif flying or waiting:
+            clock = max(clock, min([flight[0] for flight in flying[:1]] + waiting))
+        elif ready:
+            clock += 0.05
         else:
-            return steps
-
-
-SLOTS = Plan(8 * CAP, 224, SKIP, YRING, YDIRECT, RING)
-LAYER = Plan(128, 80, SKIP, YDIRECT, YRING, SKIP)
+            return steps, clock
+
+
+NEAR = ((0, 0), (0, 1), (1, 0), (1, 1), (3, 0), (3, 1), (2, 0), (2, 1))
+PLACES = (range(0, 5), range(5, 8))
+SLOTS = [
+    Plan(0, 240, 240, HALFSKIP, YRING, YDIRECT, RING),
+    Plan(240, 144, 0, HALFSKIP, YRING, YDIRECT, RING),
+]
+LAYER = [Plan(0, 128, 80, SKIP, YDIRECT, YRING, SKIP)]
 SLOT_STEPS = schedule(
-    SLOTS, True, (0.45, 0.2, 0.25, 0.06), (("aux", 1.0, 1.0), ("gram", 7.0, 0.1))
-)
-LAYER_STEPS = schedule(LAYER, False, (0.15, 0.0, 0.0, 0.0))
+    SLOTS, (0.0, 1.3), True, (0.45, 0.2, 0.25, 0.05), 1.0, (("aux", 7.0, 1.0), ("gram", 15.0, 0.1))
+)[0]
+LAYER_STEPS = schedule(LAYER, (0.0,), False, (0.15, 0.0, 0.0, 0.0), 99.0)[0]
 
 
 def layer_kernel(
     tok_hbm, routes_hbm, router_hbm, wg_hbm, wu_hbm, wd_hbm, ad_hbm, up_hbm, bound_ref,
     layer_hbm, adapted_ref, factor_ref,
-    tok_ref, routes_ref, router_ref, up_ref, w, wd, ad, tok_s, tok_y, tok_z, aux_s, aux_y, aux_z, gall, lgp, tcol, pm, whi, wlo,
-    pks, buf, acc, hid, vb, rb, rx, lbuf, gram, adp,
+    tok_ref, routes_ref, router_ref, up_ref, w, wd, ad, tok_s, tok_y, tok_z, aux_s, aux_y, aux_z, gall, lgp, tcol, pm, wsplit,
+    pks, buf, acc, hid, vb, rb, rx, lbuf, sums,
     in_sem, out_sem, w_sem, a1s, a1r, a2s, a2r, b1s, b1r, b2s, b2r, g1s, g1r, g2s, g2r,
     xs, xr, ys, yr, ags, agr, rss, rsr, lgs, lgr,
 ):
@@ -186,16 +208,23 @@
     def ffn(dz, dy):
         return {"ffn": at(dz, dy)}
 
-    def peer(d):
-        return {"expert": lax.rem(e + d, E)}
+    def expert_at(dx, dc):
+        core = lax.rem(e, 2)
+        return lax.rem(e // 2 + dx, 4) * 2 + (1 - core if dc else core)
+
+    def peer(dx, dc):
+        return {"expert": expert_at(dx, dc)}
+
+    def back(dx, dc):
+        return NEAR.index(((4 - dx) % 4, dc))
 
     barrier = pltpu.get_barrier_semaphore()
     for dy in range(1, NY):
         pl.semaphore_signal(barrier, inc=1, device_id=ffn(0, dy), device_id_type=MESH)
     for dz in range(1, NZ):
         pl.semaphore_signal(barrier, inc=1, device_id=ffn(dz, 0), device_id_type=MESH)
-    for d in range(1, E):
-        pl.semaphore_signal(barrier, inc=1, device_id=peer(d), device_id_type=MESH)
+    for d in NEAR[1:]:
+        pl.semaphore_signal(barrier, inc=1, device_id=peer(*d), device_id_type=MESH)
 
     small = [
         pltpu.make_async_copy(src, dst, in_sem.at[i])
@@ -287,17 +316,24 @@
     def slot_rows(c):
         return pl.ds(pl.multiple_of(c * CAP, 16), CAP)
 
-    for d in (4, 3, 5, 2, 6, 1, 7):
-        send(pks.at[lax.rem(e + d, E)], buf.at[f, slot_rows(e)], xs.at[d], xr.at[d], peer(d))
-    buf[f, slot_rows(e), :] = pks[e]
+    def place_rows(p):
+        return pl.ds(p * CAP, CAP)
+
+    for d in NEAR[:0:-1]:
+        p = back(*d)
+        send(pks.at[expert_at(*d)], buf.at[f, place_rows(p)], xs.at[p], xr.at[p], peer(*d))
+    buf[f, 0:CAP, :] = pks[e]
     for dz in range(1, NZ):
         send(aux_y.at[:, layer_of(dz)], aux_z.at[z], b2s.at[dz], b2r.at[dz], ffn(dz, 0))
     for i in range(NY):
         aux_z[z, i] = aux_y[i, z]
     for load in late_loads:
         load.start()
-    for d in (1, 7, 2, 6, 3, 5, 4):
-        receive(buf.at[f, slot_rows(lax.rem(e + E - d, E))], xs.at[d], xr.at[d], peer(d))
+
+    def arrive(h):
+        for p in PLACES[h]:
+            if p:
+                receive(buf.at[f, place_rows(p)], xs.at[p], xr.at[p], peer(*NEAR[p]))
 
     def aux_part():
         for dz in range(1, NZ):
@@ -326,8 +362,8 @@
             axis=1,
         )
         high = turned.astype(bf16)
-        whi[...] = high
-        wlo[...] = (turned - high.astype(f32)).astype(bf16)
+        wsplit[0:128, :] = high
+        wsplit[128:256, :] = (turned - high.astype(f32)).astype(bf16)
 
     def gram_part():
         for dz in range(1, NZ):
@@ -335,35 +371,55 @@
         for dy in range(1, NY):
             send(gall.at[y], gall.at[y], g2s.at[dy], g2r.at[dy], ffn(0, dy))
 
-    def gather_send(plan, ref, sems, key):
+    opened = set()
+
+    def gather_send(plans, ref, sems, h, key):
+        plan = plans[h]
         step, block, (r0, n) = plan.msgs[key]
         view = ref.at[at(*block), pl.ds(r0, n)]
-        i = plan.index[key]
+        i = plan.index[key] + sum(len(q.keys) for q in plans[:h])
         send(view, view, sems[0].at[i], sems[1].at[i], ffn(*step))
 
-    def gather_receive(plan, ref, sems, key):
+    def gather_receive(plans, ref, sems, h, key):
+        plan = plans[h]
         step, _, (r0, n) = plan.msgs[key]
         view = ref.at[at(*plan.target(key)), pl.ds(r0, n)]
-        i = plan.index[key]
+        i = plan.index[key] + sum(len(q.keys) for q in plans[:h])
         receive(view, sems[0].at[i], sems[1].at[i], ffn(*step))
 
-    def reduce_send(plan, key):
+    def reduce_rows(h, key):
+        plan = SLOTS[h]
+        return pl.ds(plan.offset[key] + sum(q.total for q in SLOTS[:h]), plan.msgs[key][2][1])
+
+    def reduce_send(h, key):
+        plan = SLOTS[h]
         step, _, (r0, n) = plan.msgs[key]
-        i = plan.index[key]
+        i = plan.index[key] + sum(len(q.keys) for q in SLOTS[:h])
         send(
-            vb.at[at(*plan.target(key)), pl.ds(r0, n)], rb.at[pl.ds(plan.offset[key], n)],
+            vb.at[at(*plan.target(key)), pl.ds(r0, n)], rb.at[reduce_rows(h, key)],
             rss.at[i], rsr.at[i], ffn(-step[0], -step[1]),
         )
 
-    def reduce_receive(plan, key):
+    def reduce_receive(h, key):
+        plan = SLOTS[h]
         step, block, (r0, n) = plan.msgs[key]
-        i = plan.index[key]
-        rows = pl.ds(plan.offset[key], n)
+        i = plan.index[key] + sum(len(q.keys) for q in SLOTS[:h])
+        rows = reduce_rows(h, key)
         receive(rb.at[rows], rss.at[i], rsr.at[i], ffn(-step[0], -step[1]))
         here = at(*block)
         vb[here, r0:r0 + n, :] = (
             vb[here, r0:r0 + n, :].astype(f32) + rb[rows, :].astype(f32)
         ).astype(bf16)
+
+    def results(h):
+        for p in reversed(PLACES[h]):
+            if p:
+                send(
+                    vb.at[f, place_rows(p)], rx.at[slot_rows(e)], ys.at[p], yr.at[p],
+                    peer(*NEAR[p]),
+                )
+            else:
+                rx[slot_rows(e), :] = vb[f, 0:CAP, :]
 
     def expand(dz, opening):
         if opening:
@@ -389,37 +445,36 @@
 
     for kind, first_arg, second_arg in SLOT_STEPS:
         if kind == "send" and first_arg == "gather":
-            gather_send(SLOTS, buf, (ags, agr), second_arg)
+            if second_arg[0] not in opened:
+                opened.add(second_arg[0])
+                arrive(second_arg[0])
+            gather_send(SLOTS, buf, (ags, agr), *second_arg)
         elif kind == "recv" and first_arg == "gather":
-            gather_receive(SLOTS, buf, (ags, agr), second_arg)
+            gather_receive(SLOTS, buf, (ags, agr), *second_arg)
         elif kind == "send":
-            reduce_send(SLOTS, second_arg)
+            reduce_send(*second_arg)
         elif kind == "recv":
-            reduce_receive(SLOTS, second_arg)
+            reduce_receive(*second_arg)
         elif kind == "dot":
             expand(first_arg, second_arg)
         elif kind == "act":
             activate()
         elif kind == "down":
             down(first_arg)
+        elif kind == "end":
+            results(first_arg)
         elif first_arg == "aux":
             aux_part()
         else:
             gram_part()
 
-    for d in (4, 3, 5, 2, 6, 1, 7):
-        send(
-            vb.at[f, slot_rows(lax.rem(e + d, E))], rx.at[slot_rows(e)],
-            ys.at[d], yr.at[d], peer(d),
-        )
-    rx[slot_rows(e), :] = vb[f, slot_rows(e), :]
     for dy in range(1, NY):
         receive(gall.at[col(-dy)], g2s.at[dy], g2r.at[dy], ffn(0, dy))
-    for d in (1, 7, 2, 6, 3, 5, 4):
-        receive(rx.at[slot_rows(lax.rem(e + E - d, E))], ys.at[d], yr.at[d], peer(d))
-    mixture = jnp.dot(whi[...], rx[...], preferred_element_type=f32) + jnp.dot(
-        wlo[...], rx[...], preferred_element_type=f32
-    )
+    for d in NEAR[1:]:
+        p = back(*d)
+        receive(rx.at[slot_rows(expert_at(*d))], ys.at[p], yr.at[p], peer(*d))
+    halves = jnp.dot(wsplit[...], rx[...], preferred_element_type=f32)
+    mixture = halves[0:128, :] + halves[128:256, :]
     layer_cols = tcol[...].astype(f32) + mixture
     lbuf[f] = jnp.transpose(layer_cols).astype(bf16)
     outs = []
@@ -431,17 +486,17 @@
         out.start()
         outs.append(out)
         block = jnp.concatenate([lbuf[zz * NY + i] for i in range(NY)], axis=0)
-        turned = (((0,), (0,)), ((), ()))
-        gram_g = lax.dot_general(block, block, turned, preferred_element_type=f32)
-        adp_g = lax.dot_general(block, ad[zz], turned, preferred_element_type=f32)
-        gram[...] = gram_g if opening else gram[...] + gram_g
-        adp[...] = adp_g if opening else adp[...] + adp_g
+        both = lax.dot_general(
+            block, jnp.concatenate([block, ad[zz]], axis=1), (((0,), (0,)), ((), ())),
+            preferred_element_type=f32,
+        )
+        sums[...] = both if opening else sums[...] + both
 
     for kind, first_arg, second_arg in LAYER_STEPS:
         if kind == "send":
-            gather_send(LAYER, lbuf, (lgs, lgr), second_arg)
+            gather_send(LAYER, lbuf, (lgs, lgr), *second_arg)
         elif kind == "recv":
-            gather_receive(LAYER, lbuf, (lgs, lgr), second_arg)
+            gather_receive(LAYER, lbuf, (lgs, lgr), *second_arg)
         else:
             contract(first_arg, second_arg)
 
@@ -449,20 +504,22 @@
         [gall[i % NY, i // NY] for i in range(NZ * NY)], axis=0
     )
     squared = jnp.sum(
-        jnp.sum(gram[...] * whole_gram, axis=1, keepdims=True), axis=0, keepdims=True
+        jnp.sum(sums[:, 0:128] * whole_gram, axis=1, keepdims=True), axis=0, keepdims=True
     )
     limit = bound_ref[0]
     norm = jnp.sqrt(jnp.maximum(squared, 0.0))
     factor_ref[...] = jnp.broadcast_to(limit / jnp.maximum(norm, limit), factor_ref.shape)
     own_cols = layer_cols.astype(bf16).astype(f32)
-    adapted_ref[...] = (own_cols + adp[...]).astype(bf16)
+    adapted_ref[...] = (own_cols + sums[:, 128:256]).astype(bf16)
     for copy in sent:
         copy.wait_send()
     for out in outs:
         out.wait()
 
 
-def grad_kernel(layer, up, factor, adapted, adapted_out, clipped_hbm, blocks, last_sem, out_sem):
+def grad_kernel(
+    layer, up, factor, adapted, adapted_out, clipped_hbm, blocks, last_sem, out_sem
+):
     last = pltpu.make_async_copy(adapted, adapted_out, last_sem)
     last.start()
     stores = []
@@ -488,7 +545,7 @@
     vmem = pl.BlockSpec(memory_space=pltpu.VMEM)
     hbm = pl.BlockSpec(memory_space=pl.ANY)
     V = pltpu.VMEM
-    n1, n2 = len(SLOTS.keys), len(LAYER.keys)
+    n1, n2 = sum(len(p.keys) for p in SLOTS), len(LAYER[0].keys)
     scratch = [
         V((4, NZ * NY * 128), bf16), V((2, 128), jnp.int32), V((E, NZ * NY * 128), bf16),
         V((128, 128), bf16),
@@ -496,10 +553,10 @@
         V((NY, NZ, 4, 128), bf16), V((NY, NZ, 4, 128), bf16), V((NZ, NY, 4, 128), bf16),
         V((NY, NZ, 8, 128), f32), V((NY, NZ, 8, 128), f32), V((NZ, NY, 8, 128), f32),
         V((NY, NZ, 4, 128), f32), V((8, 128), f32),
-        V((128, 128), bf16), V((R, 128), f32), V((128, R), bf16), V((128, R), bf16),
+        V((128, 128), bf16), V((R, 128), f32), V((256, R), bf16),
         V((E, CAP, 128), bf16), V((F, R, 128), bf16), V((2, R, 384), f32), V((R, 384), bf16),
-        V((F, R, 128), bf16), V((SLOTS.total, 128), bf16), V((R, 128), bf16),
-        V((F, 128, 128), bf16), V((128, 128), f32), V((128, 128), f32),
+        V((F, R, 128), bf16), V((sum(p.total for p in SLOTS), 128), bf16), V((R, 128), bf16),
+        V((F, 128, 128), bf16), V((128, 256), f32),
         dma((4,)), dma((NZ,)), dma((4, NZ)),
         dma((NY,)), dma((NY,)), dma((NZ,)), dma((NZ,)),
         dma((NY,)), dma((NY,)), dma((NZ,)), dma((NZ,)),

time: 95.7 us -> 93.6 us (0.978)
  Pallas kernels: 94.3 us -> 92.2 us
    pallas_call x1, Pallas kernels: 93 us -> 90.9 us  [per_device(): pl.pallas_call(layer_kernel, out_shape=(jax.ShapeDtypeStruct((F, 128, 128...]
where the time goes in v4:
time: 93.6 us; the launch traced here: 93.5 us
  Pallas kernels  92.2 us (99%)
  between operations  1.3 us (1%)
    pallas_call x1, Pallas kernels, per_device(): pl.pallas_call(layer_kernel, out_shape=(jax.ShapeDtypeStruct((F, 128, 128...  90.9 us

profile of v4, /device:TPU:2, one launch (start us, length us, event | category | flops | bytes accessed | tf_op | source)
XLA Modules:
  0.0 93.5 jit_solution(14094746798696982365)
XLA Ops:
  1.3 0.0 copy-start
  1.3 90.9 %shard_map.104 = (bf16[32,128,128]{2,1,0:T(8,128)(2,1)S(1)}, bf16[128,128]{1,0:T(8,128)(2,1)S(1)}, f32[8,128]{1,0:T(8,128)S(1)}) custom-call(bf16[4,4096]{1,0:T(4,128)(2,1)} %bitcast.19, s32[2,128]{1,0:T(2,128)} %bitcast.20, bf16[8,4096]{1,0:T(8,128)(2,1)} %bitcast.18, bf16[4096,384]{1,0:T(8,128)(2,1)} %bitcast.14, bf16[4096,384]{1,0:T(8,128)(2,1)} %bitcast.15, ...), custom_call_target="tpu_custom_call" | custom-call | tf_op jit(solution)/shard_map/pallas_call | solution.py:567
  92.2 0.0 copy-done
  92.2 1.3 %shard_map.105 = (bf16[128,128]{1,0:T(8,128)(2,1)}, bf16[4096,128]{1,0:T(8,128)(2,1)}) custom-call(bf16[32,128,128]{2,1,0:T(8,128)(2,1)S(1)} %get-tuple-element.7.layer, bf16[128,128]{1,0:T(8,128)(2,1)S(1)} %bitcast.13, f32[8,128]{1,0:T(8,128)S(1)} %get-tuple-element.8.factor, bf16[128,128]{1,0:T(8,128)(2,1)S(1)} %get-tuple-element.9.adapted), custom_call_target="tpu_custom_call" | custom-call | tf_op jit(solution)/shard_map/pallas_call | solution.py:587
Async XLA Ops:
  1.3 90.9 %copy-start = (bf16[1,128,128]{2,1,0:T(8,128)(2,1)S(1)}, bf16[1,128,128]{2,1,0:T(8,128)(2,1)}, u32[]{:S(2)}) copy-start(bf16[1,128,128]{2,1,0:T(8,128)(2,1)} %param.16) | copy-start | bytes 98308

commit v5 on v4

--- a/solution.py
+++ b/solution.py
@@ -169,9 +169,9 @@
     Plan(0, 240, 240, HALFSKIP, YRING, YDIRECT, RING),
     Plan(240, 144, 0, HALFSKIP, YRING, YDIRECT, RING),
 ]
-LAYER = [Plan(0, 128, 80, SKIP, YDIRECT, YRING, SKIP)]
+LAYER = [Plan(0, 128, 64, SKIP, YDIRECT, YDIRECT, SKIP)]
 SLOT_STEPS = schedule(
-    SLOTS, (0.0, 1.3), True, (0.45, 0.2, 0.25, 0.05), 1.0, (("aux", 7.0, 1.0), ("gram", 15.0, 0.1))
+    SLOTS, (0.0, 1.3), True, (0.3, 0.15, 0.2, 0.03), 1.0, (("aux", 7.0, 1.0), ("gram", 15.0, 0.1))
 )[0]
 LAYER_STEPS = schedule(LAYER, (0.0,), False, (0.15, 0.0, 0.0, 0.0), 99.0)[0]
 

time: 93.6 us -> 93 us (level)
  no operation moved by 1% of the time
where the time goes in v5:
time: 93 us; the launch traced here: 92.8 us
  Pallas kernels  91.5 us (98%)
  between operations  1.3 us (1%)
    pallas_call x1, Pallas kernels, per_device(): pl.pallas_call(layer_kernel, out_shape=(jax.ShapeDtypeStruct((F, 128, 128...  90.3 us

profile of v5, /device:TPU:2, one launch (start us, length us, event | category | flops | bytes accessed | tf_op | source)
XLA Modules:
  0.0 92.8 jit_solution(7865048646113818373)
XLA Ops:
  1.3 0.0 copy-start
  1.3 90.3 %shard_map.104 = (bf16[32,128,128]{2,1,0:T(8,128)(2,1)S(1)}, bf16[128,128]{1,0:T(8,128)(2,1)S(1)}, f32[8,128]{1,0:T(8,128)S(1)}) custom-call(bf16[4,4096]{1,0:T(4,128)(2,1)} %bitcast.19, s32[2,128]{1,0:T(2,128)} %bitcast.20, bf16[8,4096]{1,0:T(8,128)(2,1)} %bitcast.18, bf16[4096,384]{1,0:T(8,128)(2,1)} %bitcast.14, bf16[4096,384]{1,0:T(8,128)(2,1)} %bitcast.15, ...), custom_call_target="tpu_custom_call" | custom-call | tf_op jit(solution)/shard_map/pallas_call | solution.py:567
  91.6 0.0 copy-done
  91.6 1.2 %shard_map.105 = (bf16[128,128]{1,0:T(8,128)(2,1)}, bf16[4096,128]{1,0:T(8,128)(2,1)}) custom-call(bf16[32,128,128]{2,1,0:T(8,128)(2,1)S(1)} %get-tuple-element.7.layer, bf16[128,128]{1,0:T(8,128)(2,1)S(1)} %bitcast.13, f32[8,128]{1,0:T(8,128)S(1)} %get-tuple-element.8.factor, bf16[128,128]{1,0:T(8,128)(2,1)S(1)} %get-tuple-element.9.adapted), custom_call_target="tpu_custom_call" | custom-call | tf_op jit(solution)/shard_map/pallas_call | solution.py:587
Async XLA Ops:
  1.3 90.3 %copy-start = (bf16[1,128,128]{2,1,0:T(8,128)(2,1)S(1)}, bf16[1,128,128]{2,1,0:T(8,128)(2,1)}, u32[]{:S(2)}) copy-start(bf16[1,128,128]{2,1,0:T(8,128)(2,1)} %param.16) | copy-start | bytes 98308
